TPU v7x, 128 devices: a whole 4x4x4 slice. The times are simulated.
128 devices in a mesh: gx: 4 (over x_hi, core), gy: 4 (over y), gz: 8 (over z, x_lo).
Axes of the slice: x: 4 (x_hi: 2, x_lo: 2; x = x_hi * 2 + x_lo), y: 4, z: 4, core: 2. Of those that a mesh axis runs over, the one named last changes fastest.
Arguments:
- field: float32 [64, 1024, 1024], P('gx', 'gy', 'gz'), may hold values from -6 to 6
- source: float32 [64, 1024, 1024], P('gx', 'gy', 'gz'), may hold values from -6 to 6
Outputs:
- smoothed: float32 [64, 1024, 1024], P('gx', 'gy', 'gz')
All inputs are finite; a program needn't handle non-finite values.
Results may differ from a plain program's by a relative error of at most 0.00002.
Values sent between devices are 32-bit elements; how exact they have to be, the bound alone decides.
A program may use at most 64 MiB of HBM per device.

v0:
```python
import functools
import itertools

import jax
import jax.numpy as jnp
from jax import lax
from jax.experimental import pallas as pl
from jax.experimental.pallas import tpu as pltpu
from jax.sharding import PartitionSpec as P

MESH = pl.DeviceIdType.MESH
SWEEPS = 3
NQ, NY, NZ = 8, 256, 128
TILES = NY // 8
TOP = 16
ROWS = NY + 2 * TOP
SIXTH = 1.0 / 6.0

EDGES = [d for d in itertools.product((-1, 0, 1), repeat=3) if sum(map(abs, d)) == 2]
FACES = [(0, 0, 1), (0, 0, -1), (0, 1, 0), (0, -1, 0), (1, 0, 0), (-1, 0, 0)]
MESSAGES = [d for d in EDGES if d[0] == 0] + [d for d in EDGES if d[0]] + FACES
Z_FACES = [(0, 0, 1), (0, 0, -1)]


def when(cond, f):
    if cond is None:
        f()
    else:
        pl.when(cond)(f)


def kernel(
    field, source, out,
    fld, src, blk, red, sred, sblk, ql, qr, qs, sql, sqr, sqs, rql, rqr,
    load_sem, store_sem, send_sem, recv_sem, ssend_sem, srecv_sem,
):
    gx, gy, gz = (lax.axis_index(a) for a in ("gx", "gy", "gz"))
    nx, ny, nz = (lax.axis_size(a) for a in ("gx", "gy", "gz"))
    low_wall, high_wall = gx == 0, gx == nx - 1

    def device(d):
        return {
            "gx": gx + d[0],
            "gy": lax.rem(gy + d[1] + ny, ny),
            "gz": lax.rem(gz + d[2] + nz, nz),
        }

    def exists(d):
        if d[0] > 0:
            return gx < nx - 1
        if d[0] < 0:
            return gx > 0
        return None

    def opposite(d):
        return tuple(-v for v in d)

    own = pl.ds(TOP, NY)

    def refs(r, d):
        dx, dy, dz = d
        if dz == 0:
            sp, dp = ((8, 0) if dx > 0 else (1, 9)) if dx else (pl.ds(1, NQ), pl.ds(1, NQ))
            sr, dr = ((TOP + NY - 8, TOP - 8) if dy > 0 else (TOP, TOP + NY)) if dy else (TOP, TOP)
            n = 8 if dy else NY
            return blk.at[r, sp, pl.ds(sr, n)], blk.at[r, dp, pl.ds(dr, n)]
        col, dst = (0, ql) if dz > 0 else (2, qr)
        if dx:
            return qs.at[r, col], dst.at[r, 0 if dx > 0 else 3, pl.ds(8, 16)]
        if dy:
            sr, dr = (8, 0) if dy > 0 else (0, 24)
            return qs.at[r, col, pl.ds(sr, 8)], dst.at[r, 1, pl.ds(dr, 8)]
        return qs.at[r, pl.ds(col, 2)], dst.at[r, pl.ds(1, 2), pl.ds(8, 16)]

    def message(r, m):
        d = MESSAGES[m]
        s, t = refs(r, d)
        return pltpu.make_async_remote_copy(
            src_ref=s, dst_ref=t, send_sem=send_sem.at[m], recv_sem=recv_sem.at[r, m],
            device_id=device(d), device_id_type=MESH,
        )

    def smessage(m):
        d = FACES[m]
        dx, dy, dz = d
        if dz:
            s, t = (sqs.at[0], sql) if dz > 0 else (sqs.at[1], sqr)
        else:
            sp, dp = ((8, 0) if dx > 0 else (1, 9)) if dx else (pl.ds(1, NQ), pl.ds(1, NQ))
            sr, dr = ((TOP + NY - 8, TOP - 8) if dy > 0 else (TOP, TOP + NY)) if dy else (TOP, TOP)
            n = 8 if dy else NY
            s, t = sred.at[sp, pl.ds(sr, n)], sred.at[dp, pl.ds(dr, n)]
        return pltpu.make_async_remote_copy(
            src_ref=s, dst_ref=t, send_sem=ssend_sem.at[m], recv_sem=srecv_sem.at[m],
            device_id=device(d), device_id_type=MESH,
        )

    def each(make, dirs, what, select=None):
        for m, d in enumerate(dirs):
            if select is not None and d not in select:
                continue
            if what == "start":
                when(exists(d), lambda m=m: make(m).start())
            elif what == "sent":
                when(exists(d), lambda m=m: make(m).wait_send())
            else:
                when(exists(opposite(d)), lambda m=m: make(m).wait_recv())

    barrier = pltpu.get_barrier_semaphore()
    for d in MESSAGES:
        when(exists(d), lambda d=d: pl.semaphore_signal(barrier, inc=1, device_id=device(d), device_id_type=MESH))

    def load(array, buffer, half, n):
        planes = pl.ds(4 * n, 4)
        return pltpu.make_async_copy(array.at[planes], buffer.at[planes], load_sem.at[half, n])

    for n in range(4):
        load(field, fld, 0, n).start()
    for n in range(4):
        load(source, src, 1, n).start()

    lane = lax.broadcasted_iota(jnp.int32, (8, NZ), 1)
    sub = lax.broadcasted_iota(jnp.int32, (8, NZ), 0)
    odd = lax.rem(lane + sub, 2) == 1
    first, last = lane == 0, lane == NZ - 1

    def roll(x, shift):
        return pltpu.roll(x, shift, 1)

    def extract(value, place, accs, cols):
        hit = lane == place
        return [
            jnp.where(hit, roll(value, lax.rem(place - c + 2 * NZ, NZ)), acc)
            for c, acc in zip(cols, accs)
        ]

    zero = jnp.zeros((ROWS, NZ), jnp.float32)
    red[0] = zero
    red[9] = zero

    def wall(pair, plane):
        for r in range(SWEEPS):
            blk[r, pair] = zero
            ql[r, plane] = jnp.zeros((32, NZ), jnp.float32)
            qr[r, plane] = jnp.zeros((32, NZ), jnp.float32)

    pl.when(low_wall)(lambda: wall(0, 0))
    pl.when(high_wall)(lambda: wall(9, 3))

    COLS = (127, 126, 0, 1)

    def pack_field(q, accs):
        accs = [list(a) for a in accs]
        for t in range(TILES):
            rows = pl.ds(8 * t, 8)
            value = jnp.where(odd, fld[2 * q, rows], fld[2 * q + 1, rows])
            blk[0, q + 1, pl.ds(TOP + 8 * t, 8)] = value
            v, a = divmod(t, 16)
            accs[v] = extract(value, 8 * a + q, accs[v], COLS)
        return tuple(tuple(a) for a in accs)

    blank = jnp.zeros((8, NZ), jnp.float32)
    accs = tuple((blank,) * 4 for _ in range(2))
    for n in range(4):
        load(field, fld, 0, n).wait()
        accs = lax.fori_loop(2 * n, 2 * n + 2, pack_field, accs)
    for v in range(2):
        for c in range(4):
            qs[0, c, pl.ds(8 * v, 8)] = accs[v][c]

    walls = jnp.where(jnp.logical_or(low_wall, high_wall), 1, 0)
    pl.semaphore_wait(barrier, len(MESSAGES) - 5 * walls)
    each(functools.partial(message, 0), MESSAGES, "start")

    def pack_source(q, accs):
        accs = [list(a) for a in accs]
        for t in range(TILES):
            rows = pl.ds(8 * t, 8)
            even_plane, odd_plane = src[2 * q, rows], src[2 * q + 1, rows]
            value = jnp.where(odd, odd_plane, even_plane)
            sred[q + 1, pl.ds(TOP + 8 * t, 8)] = value
            sblk[q, rows] = jnp.where(odd, even_plane, odd_plane)
            v, a = divmod(t, 16)
            accs[v] = extract(value, 8 * a + q, accs[v], (127, 0))
        return tuple(tuple(a) for a in accs)

    accs = tuple((blank,) * 2 for _ in range(2))
    for n in range(4):
        load(source, src, 1, n).wait()
        accs = lax.fori_loop(2 * n, 2 * n + 2, pack_source, accs)
    for v in range(2):
        for c in range(2):
            sqs[c, pl.ds(8 * v, 8)] = accs[v][c]
    each(smessage, FACES, "start")

    def column(r, side, edges):
        q, s, o, near = (ql, sql, rql, 2) if side == 0 else (qr, sqr, rqr, 0)
        turned = lax.rem(sub + (1 - side), 2) == 1
        for v in range(2):
            here = pl.ds(8 * v + 8, 8)
            c = q[r, 1, here]
            before = q[r, 1, pl.ds(8 * v, 8)] if edges or v == 1 else c
            after = q[r, 1, pl.ds(8 * v + 16, 8)] if edges or v == 0 else c
            wrap = jnp.where(lane < 8, roll(before, 8), roll(c, 8))
            total = c + jnp.where(sub == 0, pltpu.roll(wrap, 1, 0), pltpu.roll(c, 1, 0))
            wrap = jnp.where(lane >= 120, roll(after, 120), roll(c, 120))
            total = total + jnp.where(sub == 7, pltpu.roll(wrap, 7, 0), pltpu.roll(c, 7, 0))
            up, down = roll(c, 127), roll(c, 1)
            if edges:
                up = jnp.where(lax.rem(lane, 8) == 7, roll(q[r, 3, here], 7), up)
                down = jnp.where(lax.rem(lane, 8) == 0, roll(q[r, 0, here], 121), down)
            total = total + jnp.where(turned, up, down)
            rows = pl.ds(8 * v, 8)
            total = total + q[r, 2, here] + qs[r, near, rows] + s[rows]
            o[rows] = total * SIXTH

    def around(ref, lead, row, left, right, place):
        c = ref[(*lead, pl.ds(row, 8))]
        total = c + ref[(*lead, pl.ds(row - 1, 8))] + ref[(*lead, pl.ds(row + 1, 8))]
        ins_left = roll(left, lax.rem(NZ - place, NZ))
        ins_right = roll(right, NZ - 1 - place)
        total = total + jnp.where(first, ins_left, roll(c, 1))
        return total + jnp.where(last, ins_right, roll(c, NZ - 1))

    def red_pair(r, q, tiles):
        plane = jnp.where(q < 0, 0, jnp.where(q > 7, 3, 1))
        slot = jnp.bitwise_and(q, 7)
        above, below = jnp.minimum(q + 2, 9), jnp.maximum(q, 0)
        for t in tiles:
            row = TOP + 8 * t
            v, a = divmod(t, 16)
            here = pl.ds(8 * v + 8, 8)
            total = around(blk, (r, q + 1), row, ql[r, plane, here], qr[r, plane, here], 8 * a + slot)
            rows = pl.ds(row, 8)
            total = total + jnp.where(odd, blk[r, above, rows], blk[r, below, rows])
            red[q + 1, rows] = (total + sred[q + 1, rows]) * SIXTH

    def black_pair(r, q, tiles, accs):
        accs = [list(a) for a in accs]
        for t in tiles:
            row = TOP + 8 * t
            v, a = divmod(t, 16)
            here = pl.ds(8 * v, 8)
            total = around(red, (q + 1,), row, rql[here], rqr[here], 8 * a + q)
            rows = pl.ds(row, 8)
            total = total + jnp.where(odd, red[q, rows], red[q + 2, rows])
            value = (total + sblk[q, pl.ds(8 * t, 8)]) * SIXTH
            blk[r + 1, q + 1, rows] = value
            accs[v] = extract(value, 8 * a + q, accs[v], COLS)
        return tuple(tuple(a) for a in accs)

    def sweep(r, carry):
        here = functools.partial(message, r)
        each(here, MESSAGES, "arrived", Z_FACES)

        @pl.when(r == 0)
        def _():
            each(smessage, FACES, "arrived", Z_FACES)

        column(r, 0, False)
        column(r, 1, False)

        def red_inner(q, c):
            red_pair(r, q, range(1, TILES - 1))
            return c

        lax.fori_loop(1, 7, red_inner, 0)
        accs = tuple((blank,) * 4 for _ in range(2))
        accs = lax.fori_loop(
            2, 6, lambda q, accs: black_pair(r, q, range(2, TILES - 2), accs), accs
        )

        rest = [d for d in MESSAGES if d not in Z_FACES]
        each(here, MESSAGES, "arrived", rest)

        @pl.when(r == 0)
        def _():
            each(smessage, FACES, "arrived", [d for d in FACES if d not in Z_FACES])

        each(here, MESSAGES, "sent")
        column(r, 0, True)
        column(r, 1, True)

        def red_outer(n, c):
            red_pair(r, n - 1 + jnp.where(n >= 2, 6, 0), range(TILES))
            return c

        lax.fori_loop(jnp.where(low_wall, 1, 0), jnp.where(high_wall, 3, 4), red_outer, 0)

        def red_ends(q, c):
            red_pair(r, q, (-1, 0, TILES - 1, TILES))
            return c

        lax.fori_loop(0, NQ, red_ends, 0)
        accs = lax.fori_loop(
            2, 6, lambda q, accs: black_pair(r, q, (0, 1, TILES - 2, TILES - 1), accs), accs
        )
        accs = lax.fori_loop(
            0, 4,
            lambda n, accs: black_pair(r, n + jnp.where(n >= 2, 4, 0), range(TILES), accs),
            accs,
        )
        for v in range(2):
            for c in range(4):
                qs[r + 1, c, pl.ds(8 * v, 8)] = accs[v][c]

        @pl.when(r < SWEEPS - 1)
        def _():
            each(functools.partial(message, r + 1), MESSAGES, "start")

        return carry

    lax.fori_loop(0, SWEEPS, sweep, 0)
    each(smessage, FACES, "sent")

    def store(q):
        planes = pl.ds(2 * q, 2)
        return pltpu.make_async_copy(fld.at[planes], out.at[planes], store_sem.at[q])

    def unpack(q, c):
        for t in range(TILES):
            rows, mine = pl.ds(TOP + 8 * t, 8), pl.ds(8 * t, 8)
            x, y = red[q + 1, rows], blk[SWEEPS, q + 1, rows]
            fld[2 * q, mine] = jnp.where(odd, y, x)
            fld[2 * q + 1, mine] = jnp.where(odd, x, y)
        store(q).start()
        return c

    lax.fori_loop(0, NQ, unpack, 0)

    def stored(q, c):
        store(q).wait()
        return c

    lax.fori_loop(0, NQ, stored, 0)


def on_device(field, source):
    f32 = jnp.float32
    dma = pltpu.SemaphoreType.DMA
    return pl.pallas_call(
        kernel,
        name="smooth",
        out_shape=jax.ShapeDtypeStruct(field.shape, f32),
        in_specs=[pl.BlockSpec(memory_space=pl.ANY)] * 2,
        out_specs=pl.BlockSpec(memory_space=pl.ANY),
        scratch_shapes=[
            pltpu.VMEM((2 * NQ, NY, NZ), f32),
            pltpu.VMEM((2 * NQ, NY, NZ), f32),
            pltpu.VMEM((SWEEPS + 1, NQ + 2, ROWS, NZ), f32),
            pltpu.VMEM((NQ + 2, ROWS, NZ), f32),
            pltpu.VMEM((NQ + 2, ROWS, NZ), f32),
            pltpu.VMEM((NQ, NY, NZ), f32),
            pltpu.VMEM((SWEEPS, 4, 32, NZ), f32),
            pltpu.VMEM((SWEEPS, 4, 32, NZ), f32),
            pltpu.VMEM((SWEEPS + 1, 4, 16, NZ), f32),
            pltpu.VMEM((16, NZ), f32),
            pltpu.VMEM((16, NZ), f32),
            pltpu.VMEM((2, 16, NZ), f32),
            pltpu.VMEM((16, NZ), f32),
            pltpu.VMEM((16, NZ), f32),
            dma((2, 4)),
            dma((NQ,)),
            dma((len(MESSAGES),)),
            dma((SWEEPS, len(MESSAGES))),
            dma((len(FACES),)),
            dma((len(FACES),)),
        ],
        compiler_params=pltpu.CompilerParams(collective_id=0, has_side_effects=True),
    )(field, source)


def solution(mesh):
    spec = P("gx", "gy", "gz")
    return jax.shard_map(
        on_device, mesh=mesh, in_specs=(spec, spec), out_specs=spec, check_vma=False
    )
```

profile of v0, /device:TPU:1, one launch (start us, length us, event | category | flops | bytes accessed | tf_op | source)
XLA Modules:
  0.0 66.0 jit_solution(291374806723660953)
XLA Ops:
  0.0 62.9 %smooth.1 = f32[16,256,128]{2,1,0:T(8,128)} custom-call(f32[16,256,128]{2,1,0:T(8,128)} %field.1, f32[16,256,128]{2,1,0:T(8,128)} %source.1), custom_call_target="tpu_custom_call" | custom-call | tf_op jit(solution)/shard_map/smooth/pallas_call | solution.py:341
  62.9 3.1 %copy.4 = f32[16,256,128]{2,1,0:T(8,128)} copy(f32[16,256,128]{2,1,0:T(8,128)} %smooth.1) | data formatting | bytes 4194304
where the time goes:
time: 66.2 us; the launch traced here: 66 us
  Pallas kernels  62.9 us (95%)
  local copies, waits for them, and re-layouts  3.11 us (5%)
    pallas_call x1, Pallas kernels, on_device(): pl.pallas_call(kernel, name='smooth', out_shape=jax.ShapeDtypeStruct(fiel...  62.9 us
    unnamed x1, local copies, waits for them, and re-layouts  3.11 us

commit v1 on v0

v1 whole, which is shorter than its diff:
```python
import functools
import itertools

import jax
import jax.numpy as jnp
from jax import lax
from jax.experimental import pallas as pl
from jax.experimental.pallas import tpu as pltpu
from jax.sharding import PartitionSpec as P

MESH = pl.DeviceIdType.MESH
SWEEPS = 3
NQ, NY, NZ = 8, 256, 128
TILES = NY // 8
TOP = 16
ROWS = NY + 2 * TOP
VECS = TILES // 8
COLS = 8 * VECS
SIXTH = 1.0 / 6.0

EDGES = [d for d in itertools.product((-1, 0, 1), repeat=3) if sum(map(abs, d)) == 2]
FACES = [(0, 0, 1), (0, 0, -1), (0, 1, 0), (0, -1, 0), (1, 0, 0), (-1, 0, 0)]
MESSAGES = [d for d in EDGES if d[0] == 0] + [d for d in EDGES if d[0]] + FACES
Z_FACES = [(0, 0, 1), (0, 0, -1)]


def when(cond, f):
    if cond is None:
        f()
    else:
        pl.when(cond)(f)


def kernel(
    field, source, out,
    fld, src, blk, red, sred, sblk, ql, qr, qlo, qhi, sql, sqr, sqlo, sqhi, ins, xins, rins,
    load_sem, store_sem, send_sem, recv_sem, ssend_sem, srecv_sem,
):
    gx, gy, gz = (lax.axis_index(a) for a in ("gx", "gy", "gz"))
    nx, ny, nz = (lax.axis_size(a) for a in ("gx", "gy", "gz"))
    low_wall, high_wall = gx == 0, gx == nx - 1

    def device(d):
        return {
            "gx": gx + d[0],
            "gy": lax.rem(gy + d[1] + ny, ny),
            "gz": lax.rem(gz + d[2] + nz, nz),
        }

    def exists(d):
        if d[0] > 0:
            return gx < nx - 1
        if d[0] < 0:
            return gx > 0
        return None

    def opposite(d):
        return tuple(-v for v in d)

    def block_slices(d):
        dx, dy, _ = d
        sp, dp = ((8, 0) if dx > 0 else (1, 9)) if dx else (pl.ds(1, NQ), pl.ds(1, NQ))
        sr, dr = ((TOP + NY - 8, TOP - 8) if dy > 0 else (TOP, TOP + NY)) if dy else (TOP, TOP)
        n = 8 if dy else NY
        return (sp, pl.ds(sr, n)), (dp, pl.ds(dr, n))

    def refs(r, d):
        dx, dy, dz = d
        if dz == 0:
            s, t = block_slices(d)
            return blk.at[(r, *s)], blk.at[(r, *t)]
        col, dst = (qhi, ql) if dz > 0 else (qlo, qr)
        own = pl.ds(8, COLS)
        if dx:
            return col.at[r], dst.at[r, 0 if dx > 0 else 2, own]
        if dy:
            sr, dr = (COLS - 8, 0) if dy > 0 else (0, COLS + 8)
            return col.at[r, pl.ds(sr, 8)], dst.at[r, 1, pl.ds(dr, 8)]
        return col.at[r], dst.at[r, 1, own]

    def message(r, m):
        d = MESSAGES[m]
        s, t = refs(r, d)
        return pltpu.make_async_remote_copy(
            src_ref=s, dst_ref=t, send_sem=send_sem.at[m], recv_sem=recv_sem.at[r, m],
            device_id=device(d), device_id_type=MESH,
        )

    def smessage(m):
        d = FACES[m]
        if d[2]:
            s, t = (sqhi, sql) if d[2] > 0 else (sqlo, sqr)
        else:
            s, t = block_slices(d)
            s, t = sred.at[s], sred.at[t]
        return pltpu.make_async_remote_copy(
            src_ref=s, dst_ref=t, send_sem=ssend_sem.at[m], recv_sem=srecv_sem.at[m],
            device_id=device(d), device_id_type=MESH,
        )

    def each(make, dirs, what, select=None):
        for m, d in enumerate(dirs):
            if select is not None and d not in select:
                continue
            if what == "start":
                when(exists(d), lambda m=m: make(m).start())
            elif what == "sent":
                when(exists(d), lambda m=m: make(m).wait_send())
            else:
                when(exists(opposite(d)), lambda m=m: make(m).wait_recv())

    barrier = pltpu.get_barrier_semaphore()
    for d in MESSAGES:
        when(exists(d), lambda d=d: pl.semaphore_signal(barrier, inc=1, device_id=device(d), device_id_type=MESH))

    def load(array, buffer, half, n):
        planes = pl.ds(4 * n, 4)
        return pltpu.make_async_copy(array.at[planes], buffer.at[planes], load_sem.at[half, n])

    for n in range(4):
        load(field, fld, 0, n).start()
    for n in range(4):
        load(source, src, 1, n).start()

    lane = lax.broadcasted_iota(jnp.int32, (8, NZ), 1)
    sub = lax.broadcasted_iota(jnp.int32, (8, NZ), 0)
    odd = jnp.bitwise_and(lane + sub, 1) == 1
    even_lane = jnp.bitwise_and(lane, 1) == 0
    first, last = lane == 0, lane == NZ - 1
    group = jnp.bitwise_and(lane, 15)
    half = jnp.right_shift(lane, 1)
    half_after = jnp.bitwise_and(half - 1, NZ // 2 - 1)

    def roll(x, shift):
        return pltpu.roll(x, shift, 1)

    def slot(t, q):
        return 8 * (t % 8) + q

    def collect(lo, hi, lead, t, q, value):
        m = slot(t, q)
        turned = roll(value, jnp.bitwise_and(2 * m + 2, NZ - 1))
        rows = pl.ds(8 * (t // 8), 8)
        hi[(*lead, rows)] = jnp.where(half == m, turned, hi[(*lead, rows)])
        lo[(*lead, rows)] = jnp.where(half_after == m, turned, lo[(*lead, rows)])

    def settle(lo, lead):
        for v in range(VECS):
            rows = pl.ds(8 * v, 8)
            lo[(*lead, rows)] = roll(lo[(*lead, rows)], NZ - 2)

    zero = jnp.zeros((ROWS, NZ), jnp.float32)

    def wall(pair, plane):
        for r in range(SWEEPS):
            blk[r, pair] = zero
            ql[r, plane] = jnp.zeros((COLS + 16, NZ), jnp.float32)
            qr[r, plane] = jnp.zeros((COLS + 16, NZ), jnp.float32)
        sred[pair] = zero

    pl.when(low_wall)(lambda: wall(0, 0))
    pl.when(high_wall)(lambda: wall(9, 2))
    inside = jnp.where(odd, jnp.where(low_wall, 0.0, SIXTH), jnp.where(high_wall, 0.0, SIXTH))

    def pack_field(q, c):
        for t in range(TILES):
            rows = pl.ds(8 * t, 8)
            value = jnp.where(odd, fld[2 * q, rows], fld[2 * q + 1, rows])
            blk[0, q + 1, pl.ds(TOP + 8 * t, 8)] = value
            collect(qlo, qhi, (0,), t, q, value)
        return c

    for n in range(4):
        load(field, fld, 0, n).wait()
        lax.fori_loop(2 * n, 2 * n + 2, pack_field, 0)
    settle(qlo, (0,))

    walls = jnp.where(jnp.logical_or(low_wall, high_wall), 1, 0)
    pl.semaphore_wait(barrier, len(MESSAGES) - 5 * walls)
    each(functools.partial(message, 0), MESSAGES, "start")

    def pack_source(q, c):
        for t in range(TILES):
            rows = pl.ds(8 * t, 8)
            even_plane, odd_plane = src[2 * q, rows], src[2 * q + 1, rows]
            value = jnp.where(odd, odd_plane, even_plane)
            sred[q + 1, pl.ds(TOP + 8 * t, 8)] = value
            sblk[q, rows] = jnp.where(odd, even_plane, odd_plane)
            collect(sqlo, sqhi, (), t, q, value)
        return c

    for n in range(4):
        load(source, src, 1, n).wait()
        lax.fori_loop(2 * n, 2 * n + 2, pack_source, 0)
    settle(sqlo, ())
    each(smessage, FACES, "start")

    def columns(r, edges):
        for v in range(-1, VECS + 1) if edges else range(VECS):
            rows = pl.ds(8 * v + 8, 8)
            ins[rows] = jnp.where(even_lane, qr[r, 1, rows], ql[r, 1, rows])
        for v in range(VECS):
            here, rows = pl.ds(8 * v + 8, 8), pl.ds(8 * v, 8)
            c = ins[here]
            before = ins[rows] if edges or v > 0 else c
            after = ins[pl.ds(8 * v + 16, 8)] if edges or v < VECS - 1 else c
            back = roll(jnp.where(lane >= NZ - 16, before, c), 16)
            ahead = roll(jnp.where(lane < 16, after, c), NZ - 16)
            total = c + jnp.where(sub == 0, pltpu.roll(back, 1, 0), pltpu.roll(c, 1, 0))
            total = total + jnp.where(sub == 7, pltpu.roll(ahead, 7, 0), pltpu.roll(c, 7, 0))
            up, down = roll(c, NZ - 2), roll(c, 2)
            if edges:
                above = jnp.where(even_lane, qr[r, 2, here], ql[r, 2, here])
                below = jnp.where(even_lane, qr[r, 0, here], ql[r, 0, here])
                up = jnp.where(group >= 14, roll(above, 14), up)
                down = jnp.where(group < 2, roll(below, NZ - 14), down)
                xins[rows] = jnp.where(odd, above, roll(below, NZ - 14))
            total = total + jnp.where(odd, up, down)
            left, right = ql[r, 1, here] + qlo[r, rows], qr[r, 1, here] + qhi[r, rows]
            total = total + jnp.where(even_lane, roll(right, NZ - 1), roll(left, 1))
            total = total + jnp.where(even_lane, sqr[rows], sql[rows])
            rins[rows] = total * SIXTH

    def beside(c, edge, m):
        edge = roll(edge, NZ - 1 - 2 * m)
        return jnp.where(first, edge, roll(c, 1)) + jnp.where(last, edge, roll(c, NZ - 1))

    def around(ref, lead, row, edge, m):
        c = ref[(*lead, pl.ds(row, 8))]
        total = c + ref[(*lead, pl.ds(row - 1, 8))] + ref[(*lead, pl.ds(row + 1, 8))]
        return total + beside(c, edge, m)

    def red_tile(r, q, t):
        rows = pl.ds(TOP + 8 * t, 8)
        total = around(blk, (r, q + 1), TOP + 8 * t, ins[pl.ds(8 * (t // 8) + 8, 8)], slot(t, q))
        total = total + jnp.where(odd, blk[r, q + 2, rows], blk[r, q, rows])
        red[q + 1, rows] = (total + sred[q + 1, rows]) * SIXTH

    def halo_tiles(r):
        for t in range(TILES):
            row = TOP + 8 * t
            rows = pl.ds(row, 8)
            low, high = blk[r, 0, rows], blk[r, 9, rows]
            c, far = jnp.where(odd, high, low), jnp.where(odd, low, high)
            total = jnp.where(odd, blk[r, 0, pl.ds(row - 1, 8)], blk[r, 9, pl.ds(row - 1, 8)])
            total = total + jnp.where(odd, blk[r, 0, pl.ds(row + 1, 8)], blk[r, 9, pl.ds(row + 1, 8)])
            total = total + beside(c, xins[pl.ds(8 * (t // 8), 8)], slot(t, 0))
            total = total + far + jnp.where(odd, blk[r, 1, rows], blk[r, 8, rows])
            total = total + jnp.where(odd, sred[0, rows], sred[9, rows])
            red[0, rows] = total * inside

    def black_tile(r, q, t, final):
        rows = pl.ds(TOP + 8 * t, 8)
        total = around(red, (q + 1,), TOP + 8 * t, rins[pl.ds(8 * (t // 8), 8)], slot(t, q))
        above = (0 if q == NQ - 1 else q + 2) if isinstance(q, int) else q + 2
        total = total + jnp.where(odd, red[q, rows], red[above, rows])
        mine = pl.ds(8 * t, 8)
        value = (total + sblk[q, mine]) * SIXTH
        if final:
            other = red[q + 1, rows]
            fld[2 * q, mine] = jnp.where(odd, value, other)
            fld[2 * q + 1, mine] = jnp.where(odd, other, value)
        else:
            blk[r + 1, q + 1, rows] = value
            collect(qlo, qhi, (r + 1,), t, q, value)

    def store(q):
        planes = pl.ds(2 * q, 2)
        return pltpu.make_async_copy(fld.at[planes], out.at[planes], store_sem.at[q])

    def sweep(r, final):
        here = functools.partial(message, r)
        each(here, MESSAGES, "arrived", Z_FACES)

        @pl.when(r == 0)
        def _():
            each(smessage, FACES, "arrived", Z_FACES)

        columns(r, False)

        def red_inner(n, c):
            for q in (2 * n + 1, 2 * n + 2):
                for t in range(1, TILES - 1):
                    red_tile(r, q, t)
            return c

        lax.fori_loop(0, 3, red_inner, 0)

        def black_inner(n, c):
            for q in (2 * n, 2 * n + 1):
                for t in range(2, TILES - 2):
                    black_tile(r, q, t, final)
            return c

        lax.fori_loop(1, 3, black_inner, 0)

        rest = [d for d in MESSAGES if d not in Z_FACES]
        each(here, MESSAGES, "arrived", rest)

        @pl.when(r == 0)
        def _():
            each(smessage, FACES, "arrived", [d for d in FACES if d not in Z_FACES])

        each(here, MESSAGES, "sent")
        columns(r, True)
        for q in (0, NQ - 1):
            for t in range(1, TILES - 1):
                red_tile(r, q, t)
        for q in range(NQ):
            for t in (-1, 0, TILES - 1, TILES):
                red_tile(r, q, t)
        halo_tiles(r)
        for q in range(2, 6):
            for t in (0, 1, TILES - 2, TILES - 1):
                black_tile(r, q, t, final)
            if final:
                store(q).start()
        for q in (0, 1, 6, 7):
            for t in range(TILES):
                black_tile(r, q, t, final)
            if final:
                store(q).start()
        if not final:
            settle(qlo, (r + 1,))
            each(functools.partial(message, r + 1), MESSAGES, "start")

    def sweeps(r, c):
        sweep(r, False)
        return c

    lax.fori_loop(0, SWEEPS - 1, sweeps, 0)
    sweep(SWEEPS - 1, True)
    each(smessage, FACES, "sent")
    for q in range(NQ):
        store(q).wait()


def on_device(field, source):
    f32 = jnp.float32
    dma = pltpu.SemaphoreType.DMA
    columns = pltpu.VMEM((COLS, NZ), f32)
    return pl.pallas_call(
        kernel,
        name="smooth",
        out_shape=jax.ShapeDtypeStruct(field.shape, f32),
        in_specs=[pl.BlockSpec(memory_space=pl.ANY)] * 2,
        out_specs=pl.BlockSpec(memory_space=pl.ANY),
        scratch_shapes=[
            pltpu.VMEM((2 * NQ, NY, NZ), f32),
            pltpu.VMEM((2 * NQ, NY, NZ), f32),
            pltpu.VMEM((SWEEPS, NQ + 2, ROWS, NZ), f32),
            pltpu.VMEM((NQ + 1, ROWS, NZ), f32),
            pltpu.VMEM((NQ + 2, ROWS, NZ), f32),
            pltpu.VMEM((NQ, NY, NZ), f32),
            pltpu.VMEM((SWEEPS, 3, COLS + 16, NZ), f32),
            pltpu.VMEM((SWEEPS, 3, COLS + 16, NZ), f32),
            pltpu.VMEM((SWEEPS, COLS, NZ), f32),
            pltpu.VMEM((SWEEPS, COLS, NZ), f32),
            columns, columns, columns, columns,
            pltpu.VMEM((COLS + 16, NZ), f32),
            columns, columns,
            dma((2, 4)),
            dma((NQ,)),
            dma((len(MESSAGES),)),
            dma((SWEEPS, len(MESSAGES))),
            dma((len(FACES),)),
            dma((len(FACES),)),
        ],
        compiler_params=pltpu.CompilerParams(collective_id=0, has_side_effects=True),
    )(field, source)


def solution(mesh):
    spec = P("gx", "gy", "gz")
    return jax.shard_map(
        on_device, mesh=mesh, in_specs=(spec, spec), out_specs=spec, check_vma=False
    )
```

time: 66.2 us -> 49.9 us (0.75)
  Pallas kernels: 62.9 us -> 46.6 us
    pallas_call x1, Pallas kernels: 62.9 us -> 46.6 us  [on_device(): pl.pallas_call(kernel, name='smooth', out_shape=jax.ShapeDtypeStruct(fiel...]
where the time goes in v1:
time: 49.9 us; the launch traced here: 49.8 us
  Pallas kernels  46.6 us (93%)
  local copies, waits for them, and re-layouts  3.11 us (6%)
    pallas_call x1, Pallas kernels, on_device(): pl.pallas_call(kernel, name='smooth', out_shape=jax.ShapeDtypeStruct(fiel...  46.6 us
    unnamed x1, local copies, waits for them, and re-layouts  3.11 us

profile of v1, /device:TPU:1, one launch (start us, length us, event | category | flops | bytes accessed | tf_op | source)
XLA Modules:
  0.0 49.8 jit_solution(10410307125155959717)
XLA Ops:
  0.0 46.6 %smooth.1 = f32[16,256,128]{2,1,0:T(8,128)} custom-call(f32[16,256,128]{2,1,0:T(8,128)} %field.1, f32[16,256,128]{2,1,0:T(8,128)} %source.1), custom_call_target="tpu_custom_call" | custom-call | tf_op jit(solution)/shard_map/smooth/pallas_call | solution.py:342
  46.6 3.1 %copy.4 = f32[16,256,128]{2,1,0:T(8,128)} copy(f32[16,256,128]{2,1,0:T(8,128)} %smooth.1) | data formatting | bytes 4194304

commit v2 on v1

--- a/solution.py
+++ b/solution.py
@@ -32,9 +32,9 @@
 
 
 def kernel(
-    field, source, out,
-    fld, src, blk, red, sred, sblk, ql, qr, qlo, qhi, sql, sqr, sqlo, sqhi, ins, xins, rins,
-    load_sem, store_sem, send_sem, recv_sem, ssend_sem, srecv_sem,
+    field, source, red, black,
+    fld, src, blk, sred, sblk, ql, qr, qlo, qhi, sql, sqr, sqlo, sqhi, ins, xins, rins,
+    load_sem, send_sem, recv_sem, ssend_sem, srecv_sem,
 ):
     gx, gy, gz = (lax.axis_index(a) for a in ("gx", "gy", "gz"))
     nx, ny, nz = (lax.axis_size(a) for a in ("gx", "gy", "gz"))
@@ -257,16 +257,13 @@
         mine = pl.ds(8 * t, 8)
         value = (total + sblk[q, mine]) * SIXTH
         if final:
-            other = red[q + 1, rows]
-            fld[2 * q, mine] = jnp.where(odd, value, other)
-            fld[2 * q + 1, mine] = jnp.where(odd, other, value)
+            black[q, mine] = value
         else:
             blk[r + 1, q + 1, rows] = value
-            collect(qlo, qhi, (r + 1,), t, q, value)
-
-    def store(q):
-        planes = pl.ds(2 * q, 2)
-        return pltpu.make_async_copy(fld.at[planes], out.at[planes], store_sem.at[q])
+
+    def collect_pair(r, q, tiles):
+        for t in tiles:
+            collect(qlo, qhi, (r,), t, q, blk[r, q + 1, pl.ds(TOP + 8 * t, 8)])
 
     def sweep(r, final):
         here = functools.partial(message, r)
@@ -293,6 +290,13 @@
             return c
 
         lax.fori_loop(1, 3, black_inner, 0)
+
+        def collect_inner(q, c):
+            collect_pair(r + 1, q, range(2, TILES - 2))
+            return c
+
+        if not final:
+            lax.fori_loop(2, 6, collect_inner, 0)
 
         rest = [d for d in MESSAGES if d not in Z_FACES]
         each(here, MESSAGES, "arrived", rest)
@@ -313,14 +317,18 @@
         for q in range(2, 6):
             for t in (0, 1, TILES - 2, TILES - 1):
                 black_tile(r, q, t, final)
-            if final:
-                store(q).start()
         for q in (0, 1, 6, 7):
             for t in range(TILES):
                 black_tile(r, q, t, final)
-            if final:
-                store(q).start()
         if not final:
+            for q in range(2, 6):
+                collect_pair(r + 1, q, (0, 1, TILES - 2, TILES - 1))
+
+            def collect_outer(n, c):
+                collect_pair(r + 1, n + jnp.where(n >= 2, 4, 0), range(TILES))
+                return c
+
+            lax.fori_loop(0, 4, collect_outer, 0)
             settle(qlo, (r + 1,))
             each(functools.partial(message, r + 1), MESSAGES, "start")
 
@@ -331,25 +339,49 @@
     lax.fori_loop(0, SWEEPS - 1, sweeps, 0)
     sweep(SWEEPS - 1, True)
     each(smessage, FACES, "sent")
-    for q in range(NQ):
+
+
+def unpack(red, black, out, buf, sem):
+    sub = lax.broadcasted_iota(jnp.int32, (8, NZ), 0)
+    odd = jnp.bitwise_and(lax.broadcasted_iota(jnp.int32, (8, NZ), 1) + sub, 1) == 1
+
+    def store(q):
+        planes = pl.ds(2 * q, 2)
+        return pltpu.make_async_copy(buf.at[planes], out.at[planes], sem.at[q])
+
+    def merge(q, c):
+        for t in range(TILES):
+            rows = pl.ds(8 * t, 8)
+            x, y = red[q + 1, pl.ds(TOP + 8 * t, 8)], black[q, rows]
+            buf[2 * q, rows] = jnp.where(odd, y, x)
+            buf[2 * q + 1, rows] = jnp.where(odd, x, y)
+        store(q).start()
+        return c
+
+    lax.fori_loop(0, NQ, merge, 0)
+
+    def stored(q, c):
         store(q).wait()
+        return c
+
+    lax.fori_loop(0, NQ, stored, 0)
 
 
 def on_device(field, source):
     f32 = jnp.float32
     dma = pltpu.SemaphoreType.DMA
     columns = pltpu.VMEM((COLS, NZ), f32)
-    return pl.pallas_call(
+    vmem = pl.BlockSpec(memory_space=pltpu.VMEM)
+    red, black = pl.pallas_call(
         kernel,
         name="smooth",
-        out_shape=jax.ShapeDtypeStruct(field.shape, f32),
+        out_shape=(pltpu.VMEM((NQ + 1, ROWS, NZ), f32), pltpu.VMEM((NQ, NY, NZ), f32)),
         in_specs=[pl.BlockSpec(memory_space=pl.ANY)] * 2,
-        out_specs=pl.BlockSpec(memory_space=pl.ANY),
+        out_specs=(vmem, vmem),
         scratch_shapes=[
             pltpu.VMEM((2 * NQ, NY, NZ), f32),
             pltpu.VMEM((2 * NQ, NY, NZ), f32),
             pltpu.VMEM((SWEEPS, NQ + 2, ROWS, NZ), f32),
-            pltpu.VMEM((NQ + 1, ROWS, NZ), f32),
             pltpu.VMEM((NQ + 2, ROWS, NZ), f32),
             pltpu.VMEM((NQ, NY, NZ), f32),
             pltpu.VMEM((SWEEPS, 3, COLS + 16, NZ), f32),
@@ -360,7 +392,6 @@
             pltpu.VMEM((COLS + 16, NZ), f32),
             columns, columns,
             dma((2, 4)),
-            dma((NQ,)),
             dma((len(MESSAGES),)),
             dma((SWEEPS, len(MESSAGES))),
             dma((len(FACES),)),
@@ -368,6 +399,15 @@
         ],
         compiler_params=pltpu.CompilerParams(collective_id=0, has_side_effects=True),
     )(field, source)
+    red, black = (pltpu.with_memory_space_constraint(x, pltpu.VMEM) for x in (red, black))
+    return pl.pallas_call(
+        unpack,
+        name="unpack",
+        out_shape=jax.ShapeDtypeStruct(field.shape, f32),
+        in_specs=[vmem, vmem],
+        out_specs=pl.BlockSpec(memory_space=pl.ANY),
+        scratch_shapes=[pltpu.VMEM((2 * NQ, NY, NZ), f32), dma((NQ,))],
+    )(red, black)
 
 
 def solution(mesh):

time: 49.9 us -> 35.7 us (0.72)
  Pallas kernels: 46.6 us -> 35.6 us
  local copies, waits for them, and re-layouts: 3.11 us -> 0 us
    pallas_call x1 -> x2, Pallas kernels: 46.6 us -> 35.6 us  [the longest x1 34.2 us: on_device(): pl.pallas_call(kernel, name='smooth', out_shape=(pltpu.VMEM((NQ + 1, ROWS...]
    unnamed x1 -> x0, local copies, waits for them, and re-layouts: 3.11 us -> none
where the time goes in v2:
time: 35.7 us; the launch traced here: 35.6 us
  Pallas kernels  35.6 us (100%)
    pallas_call x1, Pallas kernels, on_device(): pl.pallas_call(kernel, name='smooth', out_shape=(pltpu.VMEM((NQ + 1, ROWS...  34.2 us
    pallas_call x1, Pallas kernels, on_device(): pl.pallas_call(unpack, name='unpack', out_shape=jax.ShapeDtypeStruct(fiel...  1.4 us

profile of v2, /device:TPU:1, one launch (start us, length us, event | category | flops | bytes accessed | tf_op | source)
XLA Modules:
  0.0 35.6 jit_solution(4362176021732553293)
XLA Ops:
  0.0 34.2 %smooth.1 = (f32[9,288,128]{2,1,0:T(8,128)S(1)}, f32[8,256,128]{2,1,0:T(8,128)S(1)}) custom-call(f32[16,256,128]{2,1,0:T(8,128)} %field.1, f32[16,256,128]{2,1,0:T(8,128)} %source.1), custom_call_target="tpu_custom_call" | custom-call | tf_op jit(solution)/shard_map/smooth/pallas_call | solution.py:375
  34.2 1.4 %unpack.1 = f32[16,256,128]{2,1,0:T(8,128)} custom-call(f32[9,288,128]{2,1,0:T(8,128)S(1)} %get-tuple-element.7.red, f32[8,256,128]{2,1,0:T(8,128)S(1)} %get-tuple-element.8.black), custom_call_target="tpu_custom_call" | custom-call | tf_op jit(solution)/shard_map/unpack/pallas_call | solution.py:403

commit v3 on v2

--- a/solution.py
+++ b/solution.py
@@ -12,6 +12,7 @@
 SWEEPS = 3
 NQ, NY, NZ = 8, 256, 128
 TILES = NY // 8
+ENDS = (0, TILES - 1)
 TOP = 16
 ROWS = NY + 2 * TOP
 VECS = TILES // 8
@@ -21,7 +22,8 @@
 EDGES = [d for d in itertools.product((-1, 0, 1), repeat=3) if sum(map(abs, d)) == 2]
 FACES = [(0, 0, 1), (0, 0, -1), (0, 1, 0), (0, -1, 0), (1, 0, 0), (-1, 0, 0)]
 MESSAGES = [d for d in EDGES if d[0] == 0] + [d for d in EDGES if d[0]] + FACES
-Z_FACES = [(0, 0, 1), (0, 0, -1)]
+X_FACES, Y_FACES, Z_FACES = FACES[4:], FACES[2:4], FACES[:2]
+YZ_EDGES, XY_EDGES, XZ_EDGES = ([d for d in EDGES if d[a] == 0] for a in (0, 2, 1))
 
 
 def when(cond, f):
@@ -33,9 +35,16 @@
 
 def kernel(
     field, source, red, black,
-    fld, src, blk, sred, sblk, ql, qr, qlo, qhi, sql, sqr, sqlo, sqhi, ins, xins, rins,
+    fld, src, blk, sred, sblk, ql, qr, qlo, qhi, elo, ehi, sql, sqr, sqlo, sqhi, ins, xins, rins, sxs, sxd, sx,
     load_sem, send_sem, recv_sem, ssend_sem, srecv_sem,
 ):
+    def load(array, buffer, half, n):
+        planes = pl.ds(2 * n, 2)
+        return pltpu.make_async_copy(array.at[planes], buffer.at[planes], load_sem.at[half, n])
+
+    for n in range(NQ):
+        load(field, fld, 0, n).start()
+
     gx, gy, gz = (lax.axis_index(a) for a in ("gx", "gy", "gz"))
     nx, ny, nz = (lax.axis_size(a) for a in ("gx", "gy", "gz"))
     low_wall, high_wall = gx == 0, gx == nx - 1
@@ -74,8 +83,8 @@
         if dx:
             return col.at[r], dst.at[r, 0 if dx > 0 else 2, own]
         if dy:
-            sr, dr = (COLS - 8, 0) if dy > 0 else (0, COLS + 8)
-            return col.at[r, pl.ds(sr, 8)], dst.at[r, 1, pl.ds(dr, 8)]
+            end, dr = (1, 0) if dy > 0 else (0, COLS + 8)
+            return (ehi if dz > 0 else elo).at[r, end], dst.at[r, 1, pl.ds(dr, 8)]
         return col.at[r], dst.at[r, 1, own]
 
     def message(r, m):
@@ -90,6 +99,9 @@
         d = FACES[m]
         if d[2]:
             s, t = (sqhi, sql) if d[2] > 0 else (sqlo, sqr)
+        elif d[0]:
+            side = 0 if d[0] > 0 else 1
+            s, t = sxs.at[side], sxd.at[side]
         else:
             s, t = block_slices(d)
             s, t = sred.at[s], sred.at[t]
@@ -113,20 +125,12 @@
     for d in MESSAGES:
         when(exists(d), lambda d=d: pl.semaphore_signal(barrier, inc=1, device_id=device(d), device_id_type=MESH))
 
-    def load(array, buffer, half, n):
-        planes = pl.ds(4 * n, 4)
-        return pltpu.make_async_copy(array.at[planes], buffer.at[planes], load_sem.at[half, n])
-
-    for n in range(4):
-        load(field, fld, 0, n).start()
-    for n in range(4):
-        load(source, src, 1, n).start()
-
     lane = lax.broadcasted_iota(jnp.int32, (8, NZ), 1)
     sub = lax.broadcasted_iota(jnp.int32, (8, NZ), 0)
     odd = jnp.bitwise_and(lane + sub, 1) == 1
     even_lane = jnp.bitwise_and(lane, 1) == 0
     first, last = lane == 0, lane == NZ - 1
+    outer = jnp.logical_or(first, last)
     group = jnp.bitwise_and(lane, 15)
     half = jnp.right_shift(lane, 1)
     half_after = jnp.bitwise_and(half - 1, NZ // 2 - 1)
@@ -137,12 +141,18 @@
     def slot(t, q):
         return 8 * (t % 8) + q
 
-    def collect(lo, hi, lead, t, q, value):
+    def collect(lo, hi, lead, t, q, value, rows=None):
         m = slot(t, q)
         turned = roll(value, jnp.bitwise_and(2 * m + 2, NZ - 1))
-        rows = pl.ds(8 * (t // 8), 8)
+        rows = pl.ds(8 * (t // 8), 8) if rows is None else rows
         hi[(*lead, rows)] = jnp.where(half == m, turned, hi[(*lead, rows)])
         lo[(*lead, rows)] = jnp.where(half_after == m, turned, lo[(*lead, rows)])
+
+    def collect_edges(r):
+        for end, t in enumerate(ENDS):
+            for q in range(NQ):
+                collect(elo, ehi, (r, end), t, q, blk[r, q + 1, pl.ds(TOP + 8 * t, 8)], pl.ds(0, 8))
+            elo[r, end] = roll(elo[r, end], NZ - 2)
 
     def settle(lo, lead):
         for v in range(VECS):
@@ -156,7 +166,7 @@
             blk[r, pair] = zero
             ql[r, plane] = jnp.zeros((COLS + 16, NZ), jnp.float32)
             qr[r, plane] = jnp.zeros((COLS + 16, NZ), jnp.float32)
-        sred[pair] = zero
+        sxd[0 if pair == 0 else 1] = jnp.zeros((NY // 2, NZ), jnp.float32)
 
     pl.when(low_wall)(lambda: wall(0, 0))
     pl.when(high_wall)(lambda: wall(9, 2))
@@ -170,9 +180,13 @@
             collect(qlo, qhi, (0,), t, q, value)
         return c
 
-    for n in range(4):
-        load(field, fld, 0, n).wait()
-        lax.fori_loop(2 * n, 2 * n + 2, pack_field, 0)
+    def packed_field(q, c):
+        load(field, fld, 0, q).wait()
+        load(source, src, 1, q).start()
+        return pack_field(q, c)
+
+    lax.fori_loop(0, NQ, packed_field, 0)
+    collect_edges(0)
     settle(qlo, (0,))
 
     walls = jnp.where(jnp.logical_or(low_wall, high_wall), 1, 0)
@@ -189,11 +203,21 @@
             collect(sqlo, sqhi, (), t, q, value)
         return c
 
-    for n in range(4):
-        load(source, src, 1, n).wait()
-        lax.fori_loop(2 * n, 2 * n + 2, pack_source, 0)
+    def packed_source(q, c):
+        load(source, src, 1, q).wait()
+        return pack_source(q, c)
+
+    def swap(x):
+        return jnp.where(jnp.bitwise_and(sub, 1) == 0, pltpu.roll(x, 7, 0), pltpu.roll(x, 1, 0))
+
+    lax.fori_loop(0, NQ, packed_source, 0)
     settle(sqlo, ())
-    each(smessage, FACES, "start")
+    each(smessage, FACES, "start", Z_FACES + Y_FACES)
+    for t in range(TILES // 2):
+        near, away = pl.ds(TOP + 8 * t, 8), pl.ds(TOP + 8 * t + NY // 2, 8)
+        sxs[0, pl.ds(8 * t, 8)] = jnp.where(odd, sred[NQ, near], swap(sred[NQ, away]))
+        sxs[1, pl.ds(8 * t, 8)] = jnp.where(odd, swap(sred[1, away]), sred[1, near])
+    each(smessage, FACES, "start", X_FACES)
 
     def columns(r, edges):
         for v in range(-1, VECS + 1) if edges else range(VECS):
@@ -231,13 +255,48 @@
         return total + beside(c, edge, m)
 
     def red_tile(r, q, t):
+        row = TOP + 8 * t
+        rows = pl.ds(row, 8)
+        c = blk[r, q + 1, rows]
+        total = c + jnp.where(first, 0.0, roll(c, 1)) + jnp.where(last, 0.0, roll(c, NZ - 1))
+        up = jnp.where(sub == 0, 0.0, pltpu.roll(c, 1, 0)) if t == 0 else blk[r, q + 1, pl.ds(row - 1, 8)]
+        down = jnp.where(sub == 7, 0.0, pltpu.roll(c, 7, 0)) if t == TILES - 1 else blk[r, q + 1, pl.ds(row + 1, 8)]
+        above = blk[r, q + 2, rows] if q < NQ - 1 else 0.0
+        below = blk[r, q, rows] if q > 0 else 0.0
+        total = total + up + down + jnp.where(odd, above, below)
+        red[q + 1, rows] = (total + sred[q + 1, rows]) * SIXTH
+
+    def complete_z(q, t):
+        rows = pl.ds(TOP + 8 * t, 8)
+        edge = roll(ins[pl.ds(8 * (t // 8) + 8, 8)], NZ - 1 - 2 * slot(t, q))
+        red[q + 1, rows] = red[q + 1, rows] + jnp.where(outer, edge, 0.0) * SIXTH
+
+    def red_beyond(r, q, t):
         rows = pl.ds(TOP + 8 * t, 8)
         total = around(blk, (r, q + 1), TOP + 8 * t, ins[pl.ds(8 * (t // 8) + 8, 8)], slot(t, q))
         total = total + jnp.where(odd, blk[r, q + 2, rows], blk[r, q, rows])
         red[q + 1, rows] = (total + sred[q + 1, rows]) * SIXTH
 
-    def halo_tiles(r):
-        for t in range(TILES):
+    def complete(r, q, t):
+        row = TOP + 8 * t
+        rows = pl.ds(row, 8)
+        more = None
+        if t == 0:
+            more = jnp.where(sub == 0, blk[r, q + 1, pl.ds(row - 1, 8)], 0.0)
+        if t == TILES - 1:
+            more = jnp.where(sub == 7, blk[r, q + 1, pl.ds(row + 1, 8)], 0.0)
+        side = None
+        if q == 0:
+            side = jnp.where(odd, 0.0, blk[r, 0, rows])
+        if q == NQ - 1:
+            side = jnp.where(odd, blk[r, 9, rows], 0.0)
+        if side is not None:
+            more = side if more is None else more + side
+        if more is not None:
+            red[q + 1, rows] = red[q + 1, rows] + more * SIXTH
+
+    def halo_tiles(r, tiles):
+        for t in tiles:
             row = TOP + 8 * t
             rows = pl.ds(row, 8)
             low, high = blk[r, 0, rows], blk[r, 9, rows]
@@ -246,8 +305,7 @@
             total = total + jnp.where(odd, blk[r, 0, pl.ds(row + 1, 8)], blk[r, 9, pl.ds(row + 1, 8)])
             total = total + beside(c, xins[pl.ds(8 * (t // 8), 8)], slot(t, 0))
             total = total + far + jnp.where(odd, blk[r, 1, rows], blk[r, 8, rows])
-            total = total + jnp.where(odd, sred[0, rows], sred[9, rows])
-            red[0, rows] = total * inside
+            red[0, rows] = (total + sx[pl.ds(8 * t, 8)]) * inside
 
     def black_tile(r, q, t, final):
         rows = pl.ds(TOP + 8 * t, 8)
@@ -261,12 +319,11 @@
         else:
             blk[r + 1, q + 1, rows] = value
 
-    def collect_pair(r, q, tiles):
-        for t in tiles:
-            collect(qlo, qhi, (r,), t, q, blk[r, q + 1, pl.ds(TOP + 8 * t, 8)])
-
     def sweep(r, final):
         here = functools.partial(message, r)
+        for q in range(NQ):
+            for t in range(TILES):
+                red_tile(r, q, t)
         each(here, MESSAGES, "arrived", Z_FACES)
 
         @pl.when(r == 0)
@@ -275,28 +332,21 @@
 
         columns(r, False)
 
-        def red_inner(n, c):
-            for q in (2 * n + 1, 2 * n + 2):
+        for q in range(NQ):
+            for t in range(TILES):
+                complete_z(q, t)
+
+        def black_inner(n, c):
+            for q in (3 * n + 1, 3 * n + 2, 3 * n + 3):
                 for t in range(1, TILES - 1):
-                    red_tile(r, q, t)
-            return c
-
-        lax.fori_loop(0, 3, red_inner, 0)
-
-        def black_inner(n, c):
-            for q in (2 * n, 2 * n + 1):
-                for t in range(2, TILES - 2):
                     black_tile(r, q, t, final)
             return c
 
-        lax.fori_loop(1, 3, black_inner, 0)
-
-        def collect_inner(q, c):
-            collect_pair(r + 1, q, range(2, TILES - 2))
-            return c
-
+        lax.fori_loop(0, 2, black_inner, 0)
         if not final:
-            lax.fori_loop(2, 6, collect_inner, 0)
+            for t in range(1, TILES - 1):
+                for q in range(1, NQ - 1):
+                    collect(qlo, qhi, (r + 1,), t, q, blk[r + 1, q + 1, pl.ds(TOP + 8 * t, 8)])
 
         rest = [d for d in MESSAGES if d not in Z_FACES]
         each(here, MESSAGES, "arrived", rest)
@@ -304,33 +354,41 @@
         @pl.when(r == 0)
         def _():
             each(smessage, FACES, "arrived", [d for d in FACES if d not in Z_FACES])
+            for t in range(TILES // 2):
+                low, high = sxd[0, pl.ds(8 * t, 8)], sxd[1, pl.ds(8 * t, 8)]
+                sx[pl.ds(8 * t, 8)] = jnp.where(odd, low, high)
+                sx[pl.ds(8 * t + NY // 2, 8)] = swap(jnp.where(odd, high, low))
 
         each(here, MESSAGES, "sent")
         columns(r, True)
+        for q in range(NQ):
+            for t in (-1, TILES):
+                red_beyond(r, q, t)
+            for t in (0, 1, TILES - 2, TILES - 1):
+                complete(r, q, t)
+        halo_tiles(r, (0, 1, TILES - 2, TILES - 1))
+        for q in range(NQ):
+            for t in ENDS:
+                black_tile(r, q, t, final)
+        after = functools.partial(message, r + 1)
+        if not final:
+            collect_edges(r + 1)
+            each(after, MESSAGES, "start", YZ_EDGES)
+            each(after, MESSAGES, "start", XY_EDGES + Y_FACES)
+        for q in (0, NQ - 1):
+            for t in range(2, TILES - 2):
+                complete(r, q, t)
+        halo_tiles(r, range(2, TILES - 2))
         for q in (0, NQ - 1):
             for t in range(1, TILES - 1):
-                red_tile(r, q, t)
-        for q in range(NQ):
-            for t in (-1, 0, TILES - 1, TILES):
-                red_tile(r, q, t)
-        halo_tiles(r)
-        for q in range(2, 6):
-            for t in (0, 1, TILES - 2, TILES - 1):
-                black_tile(r, q, t, final)
-        for q in (0, 1, 6, 7):
-            for t in range(TILES):
                 black_tile(r, q, t, final)
         if not final:
-            for q in range(2, 6):
-                collect_pair(r + 1, q, (0, 1, TILES - 2, TILES - 1))
-
-            def collect_outer(n, c):
-                collect_pair(r + 1, n + jnp.where(n >= 2, 4, 0), range(TILES))
-                return c
-
-            lax.fori_loop(0, 4, collect_outer, 0)
+            for t in range(TILES):
+                for q in range(NQ) if t in ENDS else (0, NQ - 1):
+                    collect(qlo, qhi, (r + 1,), t, q, blk[r + 1, q + 1, pl.ds(TOP + 8 * t, 8)])
             settle(qlo, (r + 1,))
-            each(functools.partial(message, r + 1), MESSAGES, "start")
+            each(after, MESSAGES, "start", XZ_EDGES + Z_FACES)
+            each(after, MESSAGES, "start", X_FACES)
 
     def sweeps(r, c):
         sweep(r, False)
@@ -388,10 +446,15 @@
             pltpu.VMEM((SWEEPS, 3, COLS + 16, NZ), f32),
             pltpu.VMEM((SWEEPS, COLS, NZ), f32),
             pltpu.VMEM((SWEEPS, COLS, NZ), f32),
+            pltpu.VMEM((SWEEPS, 2, 8, NZ), f32),
+            pltpu.VMEM((SWEEPS, 2, 8, NZ), f32),
             columns, columns, columns, columns,
             pltpu.VMEM((COLS + 16, NZ), f32),
             columns, columns,
-            dma((2, 4)),
+            pltpu.VMEM((2, NY // 2, NZ), f32),
+            pltpu.VMEM((2, NY // 2, NZ), f32),
+            pltpu.VMEM((NY, NZ), f32),
+            dma((2, NQ)),
             dma((len(MESSAGES),)),
             dma((SWEEPS, len(MESSAGES))),
             dma((len(FACES),)),

time: 35.7 us -> 32.8 us (0.919)
  Pallas kernels: 35.6 us -> 32.6 us
    pallas_call x1, Pallas kernels: 34.2 us -> 31.2 us  [on_device(): pl.pallas_call(kernel, name='smooth', out_shape=(pltpu.VMEM((NQ + 1, ROWS...]
where the time goes in v3:
time: 32.8 us; the launch traced here: 32.6 us
  Pallas kernels  32.6 us (99%)
    pallas_call x1, Pallas kernels, on_device(): pl.pallas_call(kernel, name='smooth', out_shape=(pltpu.VMEM((NQ + 1, ROWS...  31.2 us
    pallas_call x1, Pallas kernels, on_device(): pl.pallas_call(unpack, name='unpack', out_shape=jax.ShapeDtypeStruct(fiel...  1.4 us

profile of v3, /device:TPU:1, one launch (start us, length us, event | category | flops | bytes accessed | tf_op | source)
XLA Modules:
  0.0 32.6 jit_solution(10516604565548440936)
XLA Ops:
  0.0 31.2 %smooth.1 = (f32[9,288,128]{2,1,0:T(8,128)S(1)}, f32[8,256,128]{2,1,0:T(8,128)S(1)}) custom-call(f32[16,256,128]{2,1,0:T(8,128)} %field.1, f32[16,256,128]{2,1,0:T(8,128)} %source.1), custom_call_target="tpu_custom_call" | custom-call | tf_op jit(solution)/shard_map/smooth/pallas_call | solution.py:433
  31.2 1.4 %unpack.1 = f32[16,256,128]{2,1,0:T(8,128)} custom-call(f32[9,288,128]{2,1,0:T(8,128)S(1)} %get-tuple-element.7.red, f32[8,256,128]{2,1,0:T(8,128)S(1)} %get-tuple-element.8.black), custom_call_target="tpu_custom_call" | custom-call | tf_op jit(solution)/shard_map/unpack/pallas_call | solution.py:466

commit v4 on v1

v4 whole, which is shorter than its diff:
```python
import functools
import itertools
import types

import jax
import jax.numpy as jnp
from jax import lax
from jax.experimental import pallas as pl
from jax.experimental.pallas import tpu as pltpu
from jax.sharding import PartitionSpec as P

MESH = pl.DeviceIdType.MESH
SWEEPS = 3
NQ, NY, NZ = 8, 256, 128
TILES = NY // 8
ENDS = (0, TILES - 1)
TOP = 16
ROWS = NY + 2 * TOP
VECS = TILES // 8
COLS = 8 * VECS
SIXTH = 1.0 / 6.0
VMEM_GRANT = 24 << 20

EDGES = [d for d in itertools.product((-1, 0, 1), repeat=3) if sum(map(abs, d)) == 2]
FACES = [(0, 0, 1), (0, 0, -1), (0, 1, 0), (0, -1, 0), (1, 0, 0), (-1, 0, 0)]
MESSAGES = [d for d in EDGES if d[0] == 0] + [d for d in EDGES if d[0]] + FACES
X_FACES, Y_FACES, Z_FACES = FACES[4:], FACES[2:4], FACES[:2]
YZ_EDGES, XY_EDGES, XZ_EDGES = ([d for d in EDGES if d[a] == 0] for a in (0, 2, 1))


def when(cond, f):
    if cond is None:
        f()
    else:
        pl.when(cond)(f)


def cells(blk, red, sred, sblk, ql, qr, qlo, qhi, sql, sqr, sx, merged, ins, xins, rins):
    gx = lax.axis_index("gx")
    low_wall, high_wall = gx == 0, gx == lax.axis_size("gx") - 1
    lane = lax.broadcasted_iota(jnp.int32, (8, NZ), 1)
    sub = lax.broadcasted_iota(jnp.int32, (8, NZ), 0)
    odd = jnp.bitwise_and(lane + sub, 1) == 1
    even_lane = jnp.bitwise_and(lane, 1) == 0
    first, last = lane == 0, lane == NZ - 1
    outer = jnp.logical_or(first, last)
    group = jnp.bitwise_and(lane, 15)
    half = jnp.right_shift(lane, 1)
    half_after = jnp.bitwise_and(half - 1, NZ // 2 - 1)

    def roll(x, shift):
        return pltpu.roll(x, shift, 1)

    def slot(t, q):
        return 8 * (t % 8) + q

    inside = jnp.where(odd, jnp.where(low_wall, 0.0, SIXTH), jnp.where(high_wall, 0.0, SIXTH))

    def swap(x):
        return jnp.where(jnp.bitwise_and(sub, 1) == 0, pltpu.roll(x, 7, 0), pltpu.roll(x, 1, 0))

    def columns(r, edges):
        for v in range(-1, VECS + 1) if edges else range(VECS):
            rows = pl.ds(8 * v + 8, 8)
            ins[rows] = jnp.where(even_lane, qr[r, 1, rows], ql[r, 1, rows])
        for v in range(VECS):
            here, rows = pl.ds(8 * v + 8, 8), pl.ds(8 * v, 8)
            c = ins[here]
            before = ins[rows] if edges or v > 0 else c
            after = ins[pl.ds(8 * v + 16, 8)] if edges or v < VECS - 1 else c
            back = roll(jnp.where(lane >= NZ - 16, before, c), 16)
            ahead = roll(jnp.where(lane < 16, after, c), NZ - 16)
            total = c + jnp.where(sub == 0, pltpu.roll(back, 1, 0), pltpu.roll(c, 1, 0))
            total = total + jnp.where(sub == 7, pltpu.roll(ahead, 7, 0), pltpu.roll(c, 7, 0))
            up, down = roll(c, NZ - 2), roll(c, 2)
            if edges:
                above = jnp.where(even_lane, qr[r, 2, here], ql[r, 2, here])
                below = jnp.where(even_lane, qr[r, 0, here], ql[r, 0, here])
                up = jnp.where(group >= 14, roll(above, 14), up)
                down = jnp.where(group < 2, roll(below, NZ - 14), down)
                xins[rows] = jnp.where(odd, above, roll(below, NZ - 14))
            total = total + jnp.where(odd, up, down)
            left, right = ql[r, 1, here] + qlo[r, rows], qr[r, 1, here] + qhi[r, rows]
            total = total + jnp.where(even_lane, roll(right, NZ - 1), roll(left, 1))
            total = total + jnp.where(even_lane, sqr[rows], sql[rows])
            rins[rows] = total * SIXTH

    def beside(c, edge, m):
        edge = roll(edge, NZ - 1 - 2 * m)
        return jnp.where(first, edge, roll(c, 1)) + jnp.where(last, edge, roll(c, NZ - 1))

    def around(ref, lead, row, edge, m):
        c = ref[(*lead, pl.ds(row, 8))]
        total = c + ref[(*lead, pl.ds(row - 1, 8))] + ref[(*lead, pl.ds(row + 1, 8))]
        return total + beside(c, edge, m)

    def red_tile(r, q, t):
        row = TOP + 8 * t
        rows = pl.ds(row, 8)
        c = blk[r, q + 1, rows]
        total = c + jnp.where(first, 0.0, roll(c, 1)) + jnp.where(last, 0.0, roll(c, NZ - 1))
        up = jnp.where(sub == 0, 0.0, pltpu.roll(c, 1, 0)) if t == 0 else blk[r, q + 1, pl.ds(row - 1, 8)]
        down = jnp.where(sub == 7, 0.0, pltpu.roll(c, 7, 0)) if t == TILES - 1 else blk[r, q + 1, pl.ds(row + 1, 8)]
        above = blk[r, q + 2, rows] if q < NQ - 1 else 0.0
        below = blk[r, q, rows] if q > 0 else 0.0
        total = total + up + down + jnp.where(odd, above, below)
        red[q + 1, rows] = (total + sred[q + 1, rows]) * SIXTH

    def complete_z(q, t):
        rows = pl.ds(TOP + 8 * t, 8)
        edge = roll(ins[pl.ds(8 * (t // 8) + 8, 8)], NZ - 1 - 2 * slot(t, q))
        red[q + 1, rows] = red[q + 1, rows] + jnp.where(outer, edge, 0.0) * SIXTH

    def red_beyond(r, q, t):
        rows = pl.ds(TOP + 8 * t, 8)
        total = around(blk, (r, q + 1), TOP + 8 * t, ins[pl.ds(8 * (t // 8) + 8, 8)], slot(t, q))
        total = total + jnp.where(odd, blk[r, q + 2, rows], blk[r, q, rows])
        red[q + 1, rows] = (total + sred[q + 1, rows]) * SIXTH

    def complete(r, q, t):
        row = TOP + 8 * t
        rows = pl.ds(row, 8)
        more = None
        if t == 0:
            more = jnp.where(sub == 0, blk[r, q + 1, pl.ds(row - 1, 8)], 0.0)
        if t == TILES - 1:
            more = jnp.where(sub == 7, blk[r, q + 1, pl.ds(row + 1, 8)], 0.0)
        side = None
        if q == 0:
            side = jnp.where(odd, 0.0, blk[r, 0, rows])
        if q == NQ - 1:
            side = jnp.where(odd, blk[r, 9, rows], 0.0)
        if side is not None:
            more = side if more is None else more + side
        if more is not None:
            red[q + 1, rows] = red[q + 1, rows] + more * SIXTH

    def halo_tiles(r, tiles):
        for t in tiles:
            row = TOP + 8 * t
            rows = pl.ds(row, 8)
            low, high = blk[r, 0, rows], blk[r, 9, rows]
            c, far = jnp.where(odd, high, low), jnp.where(odd, low, high)
            total = jnp.where(odd, blk[r, 0, pl.ds(row - 1, 8)], blk[r, 9, pl.ds(row - 1, 8)])
            total = total + jnp.where(odd, blk[r, 0, pl.ds(row + 1, 8)], blk[r, 9, pl.ds(row + 1, 8)])
            total = total + beside(c, xins[pl.ds(8 * (t // 8), 8)], slot(t, 0))
            total = total + far + jnp.where(odd, blk[r, 1, rows], blk[r, 8, rows])
            red[0, rows] = (total + sx[pl.ds(8 * t, 8)]) * inside

    def black_tile(r, q, t, final):
        rows = pl.ds(TOP + 8 * t, 8)
        total = around(red, (q + 1,), TOP + 8 * t, rins[pl.ds(8 * (t // 8), 8)], slot(t, q))
        above = (0 if q == NQ - 1 else q + 2) if isinstance(q, int) else q + 2
        total = total + jnp.where(odd, red[q, rows], red[above, rows])
        mine = pl.ds(8 * t, 8)
        value = (total + sblk[q, mine]) * SIXTH
        if final:
            other = red[q + 1, rows]
            merged[2 * q, mine] = jnp.where(odd, value, other)
            merged[2 * q + 1, mine] = jnp.where(odd, other, value)
        else:
            blk[r + 1, q + 1, rows] = value

    def finish_ends(r, final):
        for q in range(NQ):
            for t in (-1, TILES):
                red_beyond(r, q, t)
            for t in (0, 1, TILES - 2, TILES - 1):
                complete(r, q, t)
        halo_tiles(r, (0, 1, TILES - 2, TILES - 1))
        for q in range(NQ):
            for t in ENDS:
                black_tile(r, q, t, final)

    def finish_sides(r, final):
        for q in (0, NQ - 1):
            for t in range(2, TILES - 2):
                complete(r, q, t)
        halo_tiles(r, range(2, TILES - 2))
        for q in (0, NQ - 1):
            for t in range(1, TILES - 1):
                black_tile(r, q, t, final)

    return types.SimpleNamespace(**locals())


def kernel(
    field, source,
    blk, red, sred, sblk, ql, qr, qlo, qhi, sql, sqr, sx, merged,
    fld, src, elo, ehi, sqlo, sqhi, ins, xins, rins, sxs, sxd,
    load_sem, send_sem, recv_sem, ssend_sem, srecv_sem,
):
    def load(array, buffer, half, n):
        planes = pl.ds(4 * n, 4)
        return pltpu.make_async_copy(array.at[planes], buffer.at[planes], load_sem.at[half, n])

    for n in range(4):
        load(field, fld, 0, n).start()

    gx, gy, gz = (lax.axis_index(a) for a in ("gx", "gy", "gz"))
    nx, ny, nz = (lax.axis_size(a) for a in ("gx", "gy", "gz"))
    low_wall, high_wall = gx == 0, gx == nx - 1

    def device(d):
        return {
            "gx": gx + d[0],
            "gy": lax.rem(gy + d[1] + ny, ny),
            "gz": lax.rem(gz + d[2] + nz, nz),
        }

    def exists(d):
        if d[0] > 0:
            return gx < nx - 1
        if d[0] < 0:
            return gx > 0
        return None

    def opposite(d):
        return tuple(-v for v in d)

    def block_slices(d):
        dx, dy, _ = d
        sp, dp = ((8, 0) if dx > 0 else (1, 9)) if dx else (pl.ds(1, NQ), pl.ds(1, NQ))
        sr, dr = ((TOP + NY - 8, TOP - 8) if dy > 0 else (TOP, TOP + NY)) if dy else (TOP, TOP)
        n = 8 if dy else NY
        return (sp, pl.ds(sr, n)), (dp, pl.ds(dr, n))

    def refs(r, d):
        dx, dy, dz = d
        if dz == 0:
            s, t = block_slices(d)
            return blk.at[(r, *s)], blk.at[(r, *t)]
        col, dst = (qhi, ql) if dz > 0 else (qlo, qr)
        own = pl.ds(8, COLS)
        if dx:
            return col.at[r], dst.at[r, 0 if dx > 0 else 2, own]
        if dy:
            end, dr = (1, 0) if dy > 0 else (0, COLS + 8)
            return (ehi if dz > 0 else elo).at[r, end], dst.at[r, 1, pl.ds(dr, 8)]
        return col.at[r], dst.at[r, 1, own]

    def side(d):
        return 1 if d[0] > 0 else 2 if d[0] < 0 else 0

    def message(r, m):
        d = MESSAGES[m]
        s, t = refs(r, d)
        group = 3 if d in Z_FACES else side(d)
        return pltpu.make_async_remote_copy(
            src_ref=s, dst_ref=t, send_sem=send_sem.at[side(d)], recv_sem=recv_sem.at[r, group],
            device_id=device(d), device_id_type=MESH,
        )

    def smessage(m):
        d = FACES[m]
        if d[2]:
            s, t = (sqhi, sql) if d[2] > 0 else (sqlo, sqr)
        elif d[0]:
            n = side(d) - 1
            s, t = sxs.at[n], sxd.at[n]
        else:
            s, t = block_slices(d)
            s, t = sred.at[s], sred.at[t]
        group = 3 if d in Z_FACES else side(d)
        return pltpu.make_async_remote_copy(
            src_ref=s, dst_ref=t, send_sem=ssend_sem.at[side(d)], recv_sem=srecv_sem.at[group],
            device_id=device(d), device_id_type=MESH,
        )

    def start(make, dirs, select):
        for m, d in enumerate(dirs):
            if d in select:
                when(exists(d), lambda m=m: make(m).start())

    def wait(sem, kib):
        some = fld.at[pl.ds(0, 2), pl.ds(0, kib)]
        pltpu.make_async_copy(some, some, sem).wait()

    SIDE_KIB = 128 + 2 * 4 + 2 * 16

    def wait_sides(sems, kib, sent):
        when(exists((1 if sent else -1, 0, 0)), lambda: wait(sems(1), kib))
        when(exists((-1 if sent else 1, 0, 0)), lambda: wait(sems(2), kib))

    def arrived_z(r):
        wait(recv_sem.at[r, 3], 2 * 16)

    def arrived_rest(r):
        wait(recv_sem.at[r, 0], 4 * 4 + 2 * 32)
        wait_sides(lambda g: recv_sem.at[r, g], SIDE_KIB, False)

    def sent():
        wait(send_sem.at[0], 4 * 4 + 2 * 16 + 2 * 32)
        wait_sides(lambda g: send_sem.at[g], SIDE_KIB, True)

    def ssent():
        wait(ssend_sem.at[0], 2 * 16 + 2 * 32)
        wait_sides(lambda g: ssend_sem.at[g], 64, True)

    barrier = pltpu.get_barrier_semaphore()
    for d in MESSAGES:
        when(exists(d), lambda d=d: pl.semaphore_signal(barrier, inc=1, device_id=device(d), device_id_type=MESH))

    w = cells(blk, red, sred, sblk, ql, qr, qlo, qhi, sql, sqr, sx, merged, ins, xins, rins)
    sub, odd, half, half_after = w.sub, w.odd, w.half, w.half_after
    roll, slot, swap = w.roll, w.slot, w.swap

    def collect(lo, hi, lead, t, q, value, rows=None):
        m = slot(t, q)
        turned = roll(value, jnp.bitwise_and(2 * m + 2, NZ - 1))
        rows = pl.ds(8 * (t // 8), 8) if rows is None else rows
        hi[(*lead, rows)] = jnp.where(half == m, turned, hi[(*lead, rows)])
        lo[(*lead, rows)] = jnp.where(half_after == m, turned, lo[(*lead, rows)])

    def collect_edges(r):
        for end, t in enumerate(ENDS):
            for q in range(NQ):
                collect(elo, ehi, (r, end), t, q, blk[r, q + 1, pl.ds(TOP + 8 * t, 8)], pl.ds(0, 8))
            elo[r, end] = roll(elo[r, end], NZ - 2)

    def settle(lo, lead):
        for v in range(VECS):
            rows = pl.ds(8 * v, 8)
            lo[(*lead, rows)] = roll(lo[(*lead, rows)], NZ - 2)

    zero = jnp.zeros((ROWS, NZ), jnp.float32)

    def wall(pair, plane):
        for r in range(SWEEPS):
            blk[r, pair] = zero
            ql[r, plane] = jnp.zeros((COLS + 16, NZ), jnp.float32)
            qr[r, plane] = jnp.zeros((COLS + 16, NZ), jnp.float32)
        sxd[0 if pair == 0 else 1] = jnp.zeros((NY // 2, NZ), jnp.float32)

    pl.when(low_wall)(lambda: wall(0, 0))
    pl.when(high_wall)(lambda: wall(9, 2))
    def pack_field(q, c):
        for t in range(TILES):
            rows = pl.ds(8 * t, 8)
            value = jnp.where(odd, fld[2 * q, rows], fld[2 * q + 1, rows])
            blk[0, q + 1, pl.ds(TOP + 8 * t, 8)] = value
            collect(qlo, qhi, (0,), t, q, value)
        return c

    def packed_field(n, c):
        load(field, fld, 0, n).wait()
        load(source, src, 1, n).start()
        return pack_field(2 * n + 1, pack_field(2 * n, c))

    lax.fori_loop(0, 4, packed_field, 0)
    collect_edges(0)
    settle(qlo, (0,))

    walls = jnp.where(jnp.logical_or(low_wall, high_wall), 1, 0)
    pl.semaphore_wait(barrier, len(MESSAGES) - 5 * walls)
    start(functools.partial(message, 0), MESSAGES, MESSAGES)

    def pack_source(q, c):
        for t in range(TILES):
            rows = pl.ds(8 * t, 8)
            even_plane, odd_plane = src[2 * q, rows], src[2 * q + 1, rows]
            value = jnp.where(odd, odd_plane, even_plane)
            sred[q + 1, pl.ds(TOP + 8 * t, 8)] = value
            sblk[q, rows] = jnp.where(odd, even_plane, odd_plane)
            collect(sqlo, sqhi, (), t, q, value)
        return c

    def packed_source(n, c):
        load(source, src, 1, n).wait()
        return pack_source(2 * n + 1, pack_source(2 * n, c))

    lax.fori_loop(0, 4, packed_source, 0)
    settle(sqlo, ())
    start(smessage, FACES, Z_FACES + Y_FACES)
    for t in range(TILES // 2):
        near, away = pl.ds(TOP + 8 * t, 8), pl.ds(TOP + 8 * t + NY // 2, 8)
        sxs[0, pl.ds(8 * t, 8)] = jnp.where(odd, sred[NQ, near], swap(sred[NQ, away]))
        sxs[1, pl.ds(8 * t, 8)] = jnp.where(odd, swap(sred[1, away]), sred[1, near])
    start(smessage, FACES, X_FACES)

    def sweep(r, final):
        for q in range(NQ):
            for t in range(TILES):
                w.red_tile(r, q, t)
        arrived_z(r)
        pl.when(r == 0)(lambda: wait(srecv_sem.at[3], 2 * 16))

        w.columns(r, False)

        for q in range(NQ):
            for t in range(TILES):
                w.complete_z(q, t)

        def black_inner(n, c):
            for q in (3 * n + 1, 3 * n + 2, 3 * n + 3):
                for t in range(1, TILES - 1):
                    w.black_tile(r, q, t, final)
            return c

        lax.fori_loop(0, 2, black_inner, 0)
        if not final:
            for t in range(1, TILES - 1):
                for q in range(1, NQ - 1):
                    collect(qlo, qhi, (r + 1,), t, q, blk[r + 1, q + 1, pl.ds(TOP + 8 * t, 8)])

        arrived_rest(r)

        @pl.when(r == 0)
        def _():
            wait(srecv_sem.at[0], 2 * 32)
            wait_sides(lambda g: srecv_sem.at[g], 64, False)
            for t in range(TILES // 2):
                low, high = sxd[0, pl.ds(8 * t, 8)], sxd[1, pl.ds(8 * t, 8)]
                sx[pl.ds(8 * t, 8)] = jnp.where(odd, low, high)
                sx[pl.ds(8 * t + NY // 2, 8)] = swap(jnp.where(odd, high, low))

        sent()
        if final:
            return
        w.columns(r, True)
        w.finish_ends(r, False)
        after = functools.partial(message, r + 1)
        collect_edges(r + 1)
        start(after, MESSAGES, YZ_EDGES + XY_EDGES + Y_FACES)
        w.finish_sides(r, False)
        for t in range(TILES):
            for q in range(NQ) if t in ENDS else (0, NQ - 1):
                collect(qlo, qhi, (r + 1,), t, q, blk[r + 1, q + 1, pl.ds(TOP + 8 * t, 8)])
        settle(qlo, (r + 1,))
        start(after, MESSAGES, XZ_EDGES + Z_FACES + X_FACES)

    def sweeps(r, c):
        sweep(r, False)
        return c

    lax.fori_loop(0, SWEEPS - 1, sweeps, 0)
    sweep(SWEEPS - 1, True)
    ssent()


def finish(
    blk, red_in, sred, sblk, ql, qr, qlo, qhi, sql, sqr, sx, merged, out, red,
    late, ins, xins, rins, sem,
):
    del red_in
    w = cells(blk, red, sred, sblk, ql, qr, qlo, qhi, sql, sqr, sx, late, ins, xins, rins)

    def store(n):
        planes, rows = [
            (pl.ds(2, 2 * NQ - 4), pl.ds(8, NY - 16)),
            (pl.ds(2, 2 * NQ - 4), pl.ds(0, 8)),
            (pl.ds(2, 2 * NQ - 4), pl.ds(NY - 8, 8)),
            (pl.ds(0, 2), pl.ds(0, NY)),
            (pl.ds(2 * NQ - 2, 2), pl.ds(0, NY)),
        ][n]
        origin = merged if n == 0 else late
        return pltpu.make_async_copy(origin.at[planes, rows], out.at[planes, rows], sem.at[n])

    store(0).start()
    r = SWEEPS - 1
    w.columns(r, True)
    w.finish_ends(r, True)
    store(1).start()
    store(2).start()
    w.finish_sides(r, True)
    store(3).start()
    store(4).start()
    for n in range(5):
        store(n).wait()


def on_device(field, source):
    f32 = jnp.float32
    dma = pltpu.SemaphoreType.DMA
    columns = (COLS, NZ)
    shared = [
        (SWEEPS, NQ + 2, ROWS, NZ),
        (NQ + 1, ROWS, NZ),
        (NQ + 2, ROWS, NZ),
        (NQ, NY, NZ),
        (SWEEPS, 3, COLS + 16, NZ),
        (SWEEPS, 3, COLS + 16, NZ),
        (SWEEPS, *columns),
        (SWEEPS, *columns),
        columns,
        columns,
        (NY, NZ),
        (2 * NQ, NY, NZ),
    ]
    vmem, hbm = (pl.BlockSpec(memory_space=m) for m in (pltpu.VMEM, pltpu.HBM))
    inserts = [pltpu.VMEM(shape, f32) for shape in ((COLS + 16, NZ), columns, columns)]
    field, source = (pltpu.with_memory_space_constraint(x, pltpu.HBM) for x in (field, source))
    state = pl.pallas_call(
        kernel,
        name="smooth",
        out_shape=[pltpu.VMEM(shape, f32) for shape in shared],
        in_specs=[hbm] * 2,
        out_specs=[vmem] * len(shared),
        scratch_shapes=[
            pltpu.VMEM((2 * NQ, NY, NZ), f32),
            pltpu.VMEM((2 * NQ, NY, NZ), f32),
            pltpu.VMEM((SWEEPS, 2, 8, NZ), f32),
            pltpu.VMEM((SWEEPS, 2, 8, NZ), f32),
            pltpu.VMEM(columns, f32),
            pltpu.VMEM(columns, f32),
            *inserts,
            pltpu.VMEM((2, NY // 2, NZ), f32),
            pltpu.VMEM((2, NY // 2, NZ), f32),
            dma((2, 4)),
            dma((3,)),
            dma((SWEEPS, 4)),
            dma((3,)),
            dma((4,)),
        ],
        compiler_params=pltpu.CompilerParams(
            collective_id=0, has_side_effects=True, vmem_limit_bytes=VMEM_GRANT
        ),
    )(field, source)
    state = [pltpu.with_memory_space_constraint(x, pltpu.VMEM) for x in state]
    result, _ = pl.pallas_call(
        finish,
        name="finish",
        out_shape=[jax.ShapeDtypeStruct(field.shape, f32), pltpu.VMEM(shared[1], f32)],
        in_specs=[vmem] * len(shared),
        out_specs=[hbm, vmem],
        input_output_aliases={1: 1},
        scratch_shapes=[pltpu.VMEM((2 * NQ, NY, NZ), f32), *inserts, dma((5,))],
        compiler_params=pltpu.CompilerParams(vmem_limit_bytes=VMEM_GRANT),
    )(*state)
    return result


def solution(mesh):
    spec = P("gx", "gy", "gz")
    return jax.shard_map(
        on_device, mesh=mesh, in_specs=(spec, spec), out_specs=spec, check_vma=False
    )
```

time: 49.9 us -> 31.5 us (0.63)
  Pallas kernels: 46.6 us -> 31.4 us
  local copies, waits for them, and re-layouts: 3.11 us -> 0 us
    pallas_call x1 -> x2, Pallas kernels: 46.6 us -> 31.4 us  [the longest x1 29.9 us: on_device(): pl.pallas_call(kernel, name='smooth', out_shape=[pltpu.VMEM(shape, f32) f...]
    unnamed x1 -> x0, local copies, waits for them, and re-layouts: 3.11 us -> none
where the time goes in v4:
time: 31.5 us; the launch traced here: 31.4 us
  Pallas kernels  31.4 us (100%)
    pallas_call x1, Pallas kernels, on_device(): pl.pallas_call(kernel, name='smooth', out_shape=[pltpu.VMEM(shape, f32) f...  29.9 us
    pallas_call x1, Pallas kernels, on_device(): pl.pallas_call(finish, name='finish', out_shape=[jax.ShapeDtypeStruct(fie...  1.51 us

profile of v4, /device:TPU:1, one launch (start us, length us, event | category | flops | bytes accessed | tf_op | source)
XLA Modules:
  0.0 31.4 jit_solution(11020211645496997087)
XLA Ops:
  0.0 29.9 %smooth.1 = (f32[3,10,288,128]{3,2,1,0:T(8,128)S(1)}, f32[9,288,128]{2,1,0:T(8,128)S(1)}, f32[10,288,128]{2,1,0:T(8,128)S(1)}, f32[8,256,128]{2,1,0:T(8,128)S(1)...) custom-call(f32[16,256,128]{2,1,0:T(8,128)} %field.1, ...), custom_call_target="tpu_custom_call" | custom-call | tf_op jit(solution)/shard_map/smooth/pallas_call | solution.py:493
  29.9 1.5 %finish.1 = (f32[16,256,128]{2,1,0:T(8,128)}, f32[9,288,128]{2,1,0:T(8,128)S(1)}) custom-call(f32[3,10,288,128]{3,2,1,0:T(8,128)S(1)} %get-tuple-element.18.blk, f32[9,288,128]{2,1,0:T(8,128)S(1)} %get-tuple-element.19.red_in, f32[10,288,128]{2,1,0:T(8,128)S(1)} %get-tuple-element.20.sred, ...), custom_call_target="tpu_custom_call", output_to_operand_aliasing={{1}: (1, {})} | custom-call | tf_op jit(solution)/shard_map/finish/pallas_call | solution.py:520

commit v5 on v4

--- a/solution.py
+++ b/solution.py
@@ -20,6 +20,7 @@
 COLS = 8 * VECS
 SIXTH = 1.0 / 6.0
 VMEM_GRANT = 24 << 20
+FIRST_ROWS = 192
 
 EDGES = [d for d in itertools.product((-1, 0, 1), repeat=3) if sum(map(abs, d)) == 2]
 FACES = [(0, 0, 1), (0, 0, -1), (0, 1, 0), (0, -1, 0), (1, 0, 0), (-1, 0, 0)]
@@ -35,7 +36,7 @@
         pl.when(cond)(f)
 
 
-def cells(blk, red, sred, sblk, ql, qr, qlo, qhi, sql, sqr, sx, merged, ins, xins, rins):
+def cells(blk, red, sred, sblk, ql, qr, xq, qlo, qhi, sql, sqr, sx, merged, ins, xins, rins):
     gx = lax.axis_index("gx")
     low_wall, high_wall = gx == 0, gx == lax.axis_size("gx") - 1
     lane = lax.broadcasted_iota(jnp.int32, (8, NZ), 1)
@@ -62,7 +63,7 @@
     def columns(r, edges):
         for v in range(-1, VECS + 1) if edges else range(VECS):
             rows = pl.ds(8 * v + 8, 8)
-            ins[rows] = jnp.where(even_lane, qr[r, 1, rows], ql[r, 1, rows])
+            ins[rows] = jnp.where(even_lane, qr[r, rows], ql[r, rows])
         for v in range(VECS):
             here, rows = pl.ds(8 * v + 8, 8), pl.ds(8 * v, 8)
             c = ins[here]
@@ -74,13 +75,15 @@
             total = total + jnp.where(sub == 7, pltpu.roll(ahead, 7, 0), pltpu.roll(c, 7, 0))
             up, down = roll(c, NZ - 2), roll(c, 2)
             if edges:
-                above = jnp.where(even_lane, qr[r, 2, here], ql[r, 2, here])
-                below = jnp.where(even_lane, qr[r, 0, here], ql[r, 0, here])
-                up = jnp.where(group >= 14, roll(above, 14), up)
-                down = jnp.where(group < 2, roll(below, NZ - 14), down)
-                xins[rows] = jnp.where(odd, above, roll(below, NZ - 14))
+                above = jnp.where(even_lane, xq[r, 1, 1], xq[r, 1, 0])
+                below = jnp.where(even_lane, xq[r, 0, 1], xq[r, 0, 0])
+                back = (NZ - 2 * v) % NZ
+                below = roll(below, back)
+                up = jnp.where(group >= 14, roll(above, 14 - 2 * v), up)
+                down = jnp.where(group < 2, below, down)
+                xins[rows] = jnp.where(odd, roll(above, back), below)
             total = total + jnp.where(odd, up, down)
-            left, right = ql[r, 1, here] + qlo[r, rows], qr[r, 1, here] + qhi[r, rows]
+            left, right = ql[r, here] + qlo[r, rows], qr[r, here] + qhi[r, rows]
             total = total + jnp.where(even_lane, roll(right, NZ - 1), roll(left, 1))
             total = total + jnp.where(even_lane, sqr[rows], sql[rows])
             rins[rows] = total * SIXTH
@@ -186,8 +189,8 @@
 
 def kernel(
     field, source,
-    blk, red, sred, sblk, ql, qr, qlo, qhi, sql, sqr, sx, merged,
-    fld, src, elo, ehi, sqlo, sqhi, ins, xins, rins, sxs, sxd,
+    blk, red, sred, sblk, ql, qr, xq, qlo, qhi, sql, sqr, sx, merged,
+    fld, src, elo, ehi, xe, sqlo, sqhi, ins, xins, rins, sxs, sxd,
     load_sem, send_sem, recv_sem, ssend_sem, srecv_sem,
 ):
     def load(array, buffer, half, n):
@@ -233,11 +236,12 @@
         col, dst = (qhi, ql) if dz > 0 else (qlo, qr)
         own = pl.ds(8, COLS)
         if dx:
-            return col.at[r], dst.at[r, 0 if dx > 0 else 2, own]
+            place = (r, 0 if dx > 0 else 1, 0 if dz > 0 else 1)
+            return xe.at[place], xq.at[place]
         if dy:
             end, dr = (1, 0) if dy > 0 else (0, COLS + 8)
-            return (ehi if dz > 0 else elo).at[r, end], dst.at[r, 1, pl.ds(dr, 8)]
-        return col.at[r], dst.at[r, 1, own]
+            return (ehi if dz > 0 else elo).at[r, end], dst.at[r, pl.ds(dr, 8)]
+        return col.at[r], dst.at[r, own]
 
     def side(d):
         return 1 if d[0] > 0 else 2 if d[0] < 0 else 0
@@ -276,7 +280,7 @@
         some = fld.at[pl.ds(0, 2), pl.ds(0, kib)]
         pltpu.make_async_copy(some, some, sem).wait()
 
-    SIDE_KIB = 128 + 2 * 4 + 2 * 16
+    SIDE_KIB = 128 + 4 * 4
 
     def wait_sides(sems, kib, sent):
         when(exists((1 if sent else -1, 0, 0)), lambda: wait(sems(1), kib))
@@ -301,7 +305,7 @@
     for d in MESSAGES:
         when(exists(d), lambda d=d: pl.semaphore_signal(barrier, inc=1, device_id=device(d), device_id_type=MESH))
 
-    w = cells(blk, red, sred, sblk, ql, qr, qlo, qhi, sql, sqr, sx, merged, ins, xins, rins)
+    w = cells(blk, red, sred, sblk, ql, qr, xq, qlo, qhi, sql, sqr, sx, merged, ins, xins, rins)
     sub, odd, half, half_after = w.sub, w.odd, w.half, w.half_after
     roll, slot, swap = w.roll, w.slot, w.swap
 
@@ -323,17 +327,26 @@
             rows = pl.ds(8 * v, 8)
             lo[(*lead, rows)] = roll(lo[(*lead, rows)], NZ - 2)
 
+    def collect_xz(r):
+        for place, pair in enumerate((NQ - 1, 0)):
+            for z, col in enumerate((qhi, qlo)):
+                piece = roll(col[r, pl.ds(0, 8)], (NZ - 2 * pair) % NZ)
+                for v in range(1, VECS):
+                    more = roll(col[r, pl.ds(8 * v, 8)], (2 * v - 2 * pair) % NZ)
+                    piece = jnp.where(jnp.right_shift(w.group, 1) == v, more, piece)
+                xe[r, place, z] = piece
+
     zero = jnp.zeros((ROWS, NZ), jnp.float32)
 
     def wall(pair, plane):
         for r in range(SWEEPS):
             blk[r, pair] = zero
-            ql[r, plane] = jnp.zeros((COLS + 16, NZ), jnp.float32)
-            qr[r, plane] = jnp.zeros((COLS + 16, NZ), jnp.float32)
+            for z in range(2):
+                xq[r, plane, z] = jnp.zeros((8, NZ), jnp.float32)
         sxd[0 if pair == 0 else 1] = jnp.zeros((NY // 2, NZ), jnp.float32)
 
     pl.when(low_wall)(lambda: wall(0, 0))
-    pl.when(high_wall)(lambda: wall(9, 2))
+    pl.when(high_wall)(lambda: wall(9, 1))
     def pack_field(q, c):
         for t in range(TILES):
             rows = pl.ds(8 * t, 8)
@@ -350,10 +363,23 @@
     lax.fori_loop(0, 4, packed_field, 0)
     collect_edges(0)
     settle(qlo, (0,))
+    collect_xz(0)
 
     walls = jnp.where(jnp.logical_or(low_wall, high_wall), 1, 0)
     pl.semaphore_wait(barrier, len(MESSAGES) - 5 * walls)
-    start(functools.partial(message, 0), MESSAGES, MESSAGES)
+    start(functools.partial(message, 0), MESSAGES, EDGES + Z_FACES + Y_FACES)
+
+    def x_face(m, row, n):
+        d = FACES[m]
+        sp, dp = (8, 0) if d[0] > 0 else (1, 9)
+        rows = pl.ds(TOP + row, n)
+        return pltpu.make_async_remote_copy(
+            src_ref=blk.at[0, sp, rows], dst_ref=blk.at[0, dp, rows],
+            send_sem=send_sem.at[side(d)], recv_sem=recv_sem.at[0, side(d)],
+            device_id=device(d), device_id_type=MESH,
+        )
+
+    start(lambda m: x_face(m, 0, FIRST_ROWS), FACES, X_FACES)
 
     def pack_source(q, c):
         for t in range(TILES):
@@ -372,6 +398,7 @@
     lax.fori_loop(0, 4, packed_source, 0)
     settle(sqlo, ())
     start(smessage, FACES, Z_FACES + Y_FACES)
+    start(lambda m: x_face(m, FIRST_ROWS, NY - FIRST_ROWS), FACES, X_FACES)
     for t in range(TILES // 2):
         near, away = pl.ds(TOP + 8 * t, 8), pl.ds(TOP + 8 * t + NY // 2, 8)
         sxs[0, pl.ds(8 * t, 8)] = jnp.where(odd, sred[NQ, near], swap(sred[NQ, away]))
@@ -427,7 +454,9 @@
             for q in range(NQ) if t in ENDS else (0, NQ - 1):
                 collect(qlo, qhi, (r + 1,), t, q, blk[r + 1, q + 1, pl.ds(TOP + 8 * t, 8)])
         settle(qlo, (r + 1,))
-        start(after, MESSAGES, XZ_EDGES + Z_FACES + X_FACES)
+        start(after, MESSAGES, Z_FACES)
+        collect_xz(r + 1)
+        start(after, MESSAGES, XZ_EDGES + X_FACES)
 
     def sweeps(r, c):
         sweep(r, False)
@@ -439,11 +468,11 @@
 
 
 def finish(
-    blk, red_in, sred, sblk, ql, qr, qlo, qhi, sql, sqr, sx, merged, out, red,
+    blk, red_in, sred, sblk, ql, qr, xq, qlo, qhi, sql, sqr, sx, merged, out, red,
     late, ins, xins, rins, sem,
 ):
     del red_in
-    w = cells(blk, red, sred, sblk, ql, qr, qlo, qhi, sql, sqr, sx, late, ins, xins, rins)
+    w = cells(blk, red, sred, sblk, ql, qr, xq, qlo, qhi, sql, sqr, sx, late, ins, xins, rins)
 
     def store(n):
         planes, rows = [
@@ -478,8 +507,9 @@
         (NQ + 1, ROWS, NZ),
         (NQ + 2, ROWS, NZ),
         (NQ, NY, NZ),
-        (SWEEPS, 3, COLS + 16, NZ),
-        (SWEEPS, 3, COLS + 16, NZ),
+        (SWEEPS, COLS + 16, NZ),
+        (SWEEPS, COLS + 16, NZ),
+        (SWEEPS, 2, 2, 8, NZ),
         (SWEEPS, *columns),
         (SWEEPS, *columns),
         columns,
@@ -501,6 +531,7 @@
             pltpu.VMEM((2 * NQ, NY, NZ), f32),
             pltpu.VMEM((SWEEPS, 2, 8, NZ), f32),
             pltpu.VMEM((SWEEPS, 2, 8, NZ), f32),
+            pltpu.VMEM((SWEEPS, 2, 2, 8, NZ), f32),
             pltpu.VMEM(columns, f32),
             pltpu.VMEM(columns, f32),
             *inserts,

time: 31.5 us -> 30.2 us (0.959)
  Pallas kernels: 31.4 us -> 30.1 us
    pallas_call x1, Pallas kernels: 29.9 us -> 28.6 us  [on_device(): pl.pallas_call(kernel, name='smooth', out_shape=[pltpu.VMEM(shape, f32) f...]
where the time goes in v5:
time: 30.2 us; the launch traced here: 30.1 us
  Pallas kernels  30.1 us (100%)
    pallas_call x1, Pallas kernels, on_device(): pl.pallas_call(kernel, name='smooth', out_shape=[pltpu.VMEM(shape, f32) f...  28.6 us
    pallas_call x1, Pallas kernels, on_device(): pl.pallas_call(finish, name='finish', out_shape=[jax.ShapeDtypeStruct(fie...  1.5 us

profile of v5, /device:TPU:1, one launch (start us, length us, event | category | flops | bytes accessed | tf_op | source)
XLA Modules:
  0.0 30.1 jit_solution(13527772266513270339)
XLA Ops:
  0.0 28.6 %smooth.1 = (f32[3,10,288,128]{3,2,1,0:T(8,128)S(1)}, f32[9,288,128]{2,1,0:T(8,128)S(1)}, f32[10,288,128]{2,1,0:T(8,128)S(1)}, f32[8,256,128]{2,1,0:T(8,128)S(1)...) custom-call(f32[16,256,128]{2,1,0:T(8,128)} %field.1, ...), custom_call_target="tpu_custom_call" | custom-call | tf_op jit(solution)/shard_map/smooth/pallas_call | solution.py:523
  28.6 1.5 %finish.1 = (f32[16,256,128]{2,1,0:T(8,128)}, f32[9,288,128]{2,1,0:T(8,128)S(1)}) custom-call(f32[3,10,288,128]{3,2,1,0:T(8,128)S(1)} %get-tuple-element.19.blk, f32[9,288,128]{2,1,0:T(8,128)S(1)} %get-tuple-element.20.red_in, f32[10,288,128]{2,1,0:T(8,128)S(1)} %get-tuple-element.21.sred, ...), custom_call_target="tpu_custom_call", output_to_operand_aliasing={{1}: (1, {})} | custom-call | tf_op jit(solution)/shard_map/finish/pallas_call | solution.py:551

commit v6 on v5

--- a/solution.py
+++ b/solution.py
@@ -20,7 +20,6 @@
 COLS = 8 * VECS
 SIXTH = 1.0 / 6.0
 VMEM_GRANT = 24 << 20
-FIRST_ROWS = 192
 
 EDGES = [d for d in itertools.product((-1, 0, 1), repeat=3) if sum(map(abs, d)) == 2]
 FACES = [(0, 0, 1), (0, 0, -1), (0, 1, 0), (0, -1, 0), (1, 0, 0), (-1, 0, 0)]
@@ -175,14 +174,16 @@
             for t in ENDS:
                 black_tile(r, q, t, final)
 
-    def finish_sides(r, final):
+    def finish_sides(r, final, ready=None):
         for q in (0, NQ - 1):
             for t in range(2, TILES - 2):
                 complete(r, q, t)
         halo_tiles(r, range(2, TILES - 2))
-        for q in (0, NQ - 1):
+        for n, q in enumerate((0, NQ - 1)):
             for t in range(1, TILES - 1):
                 black_tile(r, q, t, final)
+            if ready is not None:
+                ready(n)
 
     return types.SimpleNamespace(**locals())
 
@@ -369,18 +370,6 @@
     pl.semaphore_wait(barrier, len(MESSAGES) - 5 * walls)
     start(functools.partial(message, 0), MESSAGES, EDGES + Z_FACES + Y_FACES)
 
-    def x_face(m, row, n):
-        d = FACES[m]
-        sp, dp = (8, 0) if d[0] > 0 else (1, 9)
-        rows = pl.ds(TOP + row, n)
-        return pltpu.make_async_remote_copy(
-            src_ref=blk.at[0, sp, rows], dst_ref=blk.at[0, dp, rows],
-            send_sem=send_sem.at[side(d)], recv_sem=recv_sem.at[0, side(d)],
-            device_id=device(d), device_id_type=MESH,
-        )
-
-    start(lambda m: x_face(m, 0, FIRST_ROWS), FACES, X_FACES)
-
     def pack_source(q, c):
         for t in range(TILES):
             rows = pl.ds(8 * t, 8)
@@ -398,7 +387,7 @@
     lax.fori_loop(0, 4, packed_source, 0)
     settle(sqlo, ())
     start(smessage, FACES, Z_FACES + Y_FACES)
-    start(lambda m: x_face(m, FIRST_ROWS, NY - FIRST_ROWS), FACES, X_FACES)
+    start(functools.partial(message, 0), MESSAGES, X_FACES)
     for t in range(TILES // 2):
         near, away = pl.ds(TOP + 8 * t, 8), pl.ds(TOP + 8 * t + NY // 2, 8)
         sxs[0, pl.ds(8 * t, 8)] = jnp.where(odd, sred[NQ, near], swap(sred[NQ, away]))
@@ -424,7 +413,8 @@
                     w.black_tile(r, q, t, final)
             return c
 
-        lax.fori_loop(0, 2, black_inner, 0)
+        black_inner(0, 0)
+        black_inner(1, 0)
         if not final:
             for t in range(1, TILES - 1):
                 for q in range(1, NQ - 1):
@@ -491,9 +481,7 @@
     w.finish_ends(r, True)
     store(1).start()
     store(2).start()
-    w.finish_sides(r, True)
-    store(3).start()
-    store(4).start()
+    w.finish_sides(r, True, lambda n: store(3 + n).start())
     for n in range(5):
         store(n).wait()
 

time: 30.2 us -> 28.9 us (0.957)
  Pallas kernels: 30.1 us -> 28.8 us
    pallas_call x1, Pallas kernels: 28.6 us -> 27.3 us  [on_device(): pl.pallas_call(kernel, name='smooth', out_shape=[pltpu.VMEM(shape, f32) f...]
where the time goes in v6:
time: 28.9 us; the launch traced here: 28.8 us
  Pallas kernels  28.8 us (100%)
    pallas_call x1, Pallas kernels, on_device(): pl.pallas_call(kernel, name='smooth', out_shape=[pltpu.VMEM(shape, f32) f...  27.3 us
    pallas_call x1, Pallas kernels, on_device(): pl.pallas_call(finish, name='finish', out_shape=[jax.ShapeDtypeStruct(fie...  1.5 us

profile of v6, /device:TPU:1, one launch (start us, length us, event | category | flops | bytes accessed | tf_op | source)
XLA Modules:
  0.0 28.8 jit_solution(12303595742007331147)
XLA Ops:
  0.0 27.3 %smooth.1 = (f32[3,10,288,128]{3,2,1,0:T(8,128)S(1)}, f32[9,288,128]{2,1,0:T(8,128)S(1)}, f32[10,288,128]{2,1,0:T(8,128)S(1)}, f32[8,256,128]{2,1,0:T(8,128)S(1)...) custom-call(f32[16,256,128]{2,1,0:T(8,128)} %field.1, ...), custom_call_target="tpu_custom_call" | custom-call | tf_op jit(solution)/shard_map/smooth/pallas_call | solution.py:511
  27.3 1.5 %finish.1 = (f32[16,256,128]{2,1,0:T(8,128)}, f32[9,288,128]{2,1,0:T(8,128)S(1)}) custom-call(f32[3,10,288,128]{3,2,1,0:T(8,128)S(1)} %get-tuple-element.19.blk, f32[9,288,128]{2,1,0:T(8,128)S(1)} %get-tuple-element.20.red_in, f32[10,288,128]{2,1,0:T(8,128)S(1)} %get-tuple-element.21.sred, ...), custom_call_target="tpu_custom_call", output_to_operand_aliasing={{1}: (1, {})} | custom-call | tf_op jit(solution)/shard_map/finish/pallas_call | solution.py:539

commit v7 on v6

--- a/solution.py
+++ b/solution.py
@@ -200,6 +200,8 @@
 
     for n in range(4):
         load(field, fld, 0, n).start()
+    for n in range(4):
+        load(source, src, 1, n).start()
 
     gx, gy, gz = (lax.axis_index(a) for a in ("gx", "gy", "gz"))
     nx, ny, nz = (lax.axis_size(a) for a in ("gx", "gy", "gz"))
@@ -358,10 +360,10 @@
 
     def packed_field(n, c):
         load(field, fld, 0, n).wait()
-        load(source, src, 1, n).start()
         return pack_field(2 * n + 1, pack_field(2 * n, c))
 
-    lax.fori_loop(0, 4, packed_field, 0)
+    for n in range(4):
+        packed_field(n, 0)
     collect_edges(0)
     settle(qlo, (0,))
     collect_xz(0)
@@ -384,7 +386,8 @@
         load(source, src, 1, n).wait()
         return pack_source(2 * n + 1, pack_source(2 * n, c))
 
-    lax.fori_loop(0, 4, packed_source, 0)
+    for n in range(4):
+        packed_source(n, 0)
     settle(sqlo, ())
     start(smessage, FACES, Z_FACES + Y_FACES)
     start(functools.partial(message, 0), MESSAGES, X_FACES)

time: 28.9 us -> 28.9 us (level)
  no operation moved by 1% of the time
where the time goes in v7:
time: 28.9 us; the launch traced here: 28.8 us
  Pallas kernels  28.8 us (100%)
    pallas_call x1, Pallas kernels, on_device(): pl.pallas_call(kernel, name='smooth', out_shape=[pltpu.VMEM(shape, f32) f...  27.3 us
    pallas_call x1, Pallas kernels, on_device(): pl.pallas_call(finish, name='finish', out_shape=[jax.ShapeDtypeStruct(fie...  1.5 us

profile of v7, /device:TPU:1, one launch (start us, length us, event | category | flops | bytes accessed | tf_op | source)
XLA Modules:
  0.0 28.8 jit_solution(9186916313040432133)
XLA Ops:
  0.0 27.3 %smooth.1 = (f32[3,10,288,128]{3,2,1,0:T(8,128)S(1)}, f32[9,288,128]{2,1,0:T(8,128)S(1)}, f32[10,288,128]{2,1,0:T(8,128)S(1)}, f32[8,256,128]{2,1,0:T(8,128)S(1)...) custom-call(f32[16,256,128]{2,1,0:T(8,128)} %field.1, ...), custom_call_target="tpu_custom_call" | custom-call | tf_op jit(solution)/shard_map/smooth/pallas_call | solution.py:514
  27.3 1.5 %finish.1 = (f32[16,256,128]{2,1,0:T(8,128)}, f32[9,288,128]{2,1,0:T(8,128)S(1)}) custom-call(f32[3,10,288,128]{3,2,1,0:T(8,128)S(1)} %get-tuple-element.19.blk, f32[9,288,128]{2,1,0:T(8,128)S(1)} %get-tuple-element.20.red_in, f32[10,288,128]{2,1,0:T(8,128)S(1)} %get-tuple-element.21.sred, ...), custom_call_target="tpu_custom_call", output_to_operand_aliasing={{1}: (1, {})} | custom-call | tf_op jit(solution)/shard_map/finish/pallas_call | solution.py:542

commit v8 on v7

--- a/solution.py
+++ b/solution.py
@@ -254,7 +254,7 @@
         s, t = refs(r, d)
         group = 3 if d in Z_FACES else side(d)
         return pltpu.make_async_remote_copy(
-            src_ref=s, dst_ref=t, send_sem=send_sem.at[side(d)], recv_sem=recv_sem.at[r, group],
+            src_ref=s, dst_ref=t, send_sem=send_sem.at[side(d)], recv_sem=recv_sem.at[r % 2, group],
             device_id=device(d), device_id_type=MESH,
         )
 
@@ -290,11 +290,11 @@
         when(exists((-1 if sent else 1, 0, 0)), lambda: wait(sems(2), kib))
 
     def arrived_z(r):
-        wait(recv_sem.at[r, 3], 2 * 16)
+        wait(recv_sem.at[r % 2, 3], 2 * 16)
 
     def arrived_rest(r):
-        wait(recv_sem.at[r, 0], 4 * 4 + 2 * 32)
-        wait_sides(lambda g: recv_sem.at[r, g], SIDE_KIB, False)
+        wait(recv_sem.at[r % 2, 0], 4 * 4 + 2 * 32)
+        wait_sides(lambda g: recv_sem.at[r % 2, g], SIDE_KIB, False)
 
     def sent():
         wait(send_sem.at[0], 4 * 4 + 2 * 16 + 2 * 32)
@@ -530,7 +530,7 @@
             pltpu.VMEM((2, NY // 2, NZ), f32),
             dma((2, 4)),
             dma((3,)),
-            dma((SWEEPS, 4)),
+            dma((2, 4)),
             dma((3,)),
             dma((4,)),
         ],

time: 28.9 us -> 28.9 us (level)
  no operation moved by 1% of the time
where the time goes in v8:
time: 28.9 us; the launch traced here: 28.8 us
  Pallas kernels  28.7 us (99%)
    pallas_call x1, Pallas kernels, on_device(): pl.pallas_call(kernel, name='smooth', out_shape=[pltpu.VMEM(shape, f32) f...  27.2 us
    pallas_call x1, Pallas kernels, on_device(): pl.pallas_call(finish, name='finish', out_shape=[jax.ShapeDtypeStruct(fie...  1.5 us

profile of v8, /device:TPU:1, one launch (start us, length us, event | category | flops | bytes accessed | tf_op | source)
XLA Modules:
  0.0 28.8 jit_solution(9310322886764739296)
XLA Ops:
  0.0 27.2 %smooth.1 = (f32[3,10,288,128]{3,2,1,0:T(8,128)S(1)}, f32[9,288,128]{2,1,0:T(8,128)S(1)}, f32[10,288,128]{2,1,0:T(8,128)S(1)}, f32[8,256,128]{2,1,0:T(8,128)S(1)...) custom-call(f32[16,256,128]{2,1,0:T(8,128)} %field.1, ...), custom_call_target="tpu_custom_call" | custom-call | tf_op jit(solution)/shard_map/smooth/pallas_call | solution.py:514
  27.3 1.5 %finish.1 = (f32[16,256,128]{2,1,0:T(8,128)}, f32[9,288,128]{2,1,0:T(8,128)S(1)}) custom-call(f32[3,10,288,128]{3,2,1,0:T(8,128)S(1)} %get-tuple-element.19.blk, f32[9,288,128]{2,1,0:T(8,128)S(1)} %get-tuple-element.20.red_in, f32[10,288,128]{2,1,0:T(8,128)S(1)} %get-tuple-element.21.sred, ...), custom_call_target="tpu_custom_call", output_to_operand_aliasing={{1}: (1, {})} | custom-call | tf_op jit(solution)/shard_map/finish/pallas_call | solution.py:542
